TPU v7x, 32 devices: a whole 2x2x4 slice. The times are simulated.
32 devices in a mesh: dp: 4 (over z), expert: 8 (over y, x, core).
Axes of the slice: x: 2, y: 2, z: 4, core: 2. Of those that a mesh axis runs over, the one named last changes fastest.
Arguments:
- tokens: bfloat16 [256, 192, 1024], P(None, ('dp', 'expert')), may hold values from -200 to 200
- grad_out: bfloat16 [256, 192, 1024], P(None, ('dp', 'expert')), may hold values from -6 to 6
- slot_out: bfloat16 [512, 192, 1024], P('expert', 'dp'), may hold values from -6 to 6
- slot_params: bfloat16 [512, 1024], P('expert'), may hold values from -2 to 2
Outputs:
- grad_tokens: bfloat16 [256, 192, 1024], P(None, ('dp', 'expert'))
- grad_slot_out: bfloat16 [512, 192, 1024], P('expert', 'dp')
- grad_params: float32 [512, 1024], P('expert', 'dp')
All inputs are finite; a program needn't handle non-finite values.
Results may differ from a plain program's by a relative error of at most 0.018.
Values may be sent and summed in bfloat16 or wider, within the bound.
A program may use at most 128 MiB of HBM per device.

v0:
```python
import functools

import jax
import jax.numpy as jnp
from jax import lax
from jax.experimental import pallas as pl
from jax.experimental.pallas import tpu as pltpu
from jax.sharding import PartitionSpec as P

BF = jnp.bfloat16
F32 = jnp.float32
GROUP = 16


def flip(index, mask, size):
    total, bit = 0, 1
    while bit < size:
        total = total + ((index // bit + mask // bit) % 2) * bit
        bit *= 2
    return total


def send_order(n, core):
    if n != 8:
        return list(range(n - 1, 0, -1))
    masks = []
    for low in range(2):
        masks += [6 + low - 4 * core, 2 + low + 2 * core, 4 + low + 2 * core]
    return masks + [1]


def rows_last(lhs, rhs):
    return lax.dot_general(lhs, rhs, (((1,), (1,)), ((), ())), preferred_element_type=F32)


def exchange_kernel(
    n, m, tok_hbm, go_hbm, so_hbm, par_hbm,
    grec, gt_out, gp_out,
    tok, go, so, par, allp, stage, rows, gs, comb, gt, acc, psend, precv, xsend, xrecv, gp,
    local_sem, p_send, p_recv, q_send, q_recv, a_send, a_recv, g_send, g_recv,
    z_send, z_recv, x_send, x_recv,
):
    me = lax.axis_index("expert")
    mz = lax.axis_index("dp")
    core = me % 2
    imgs = tok.shape[0]
    own = par.shape[0]
    all_img = so.shape[1]
    cols = allp.shape[1] // m
    width = allp.shape[1]
    slots = allp.shape[0]
    my_cols = pl.ds(pl.multiple_of(mz * cols, 128), cols)
    my_rows = pl.ds(pl.multiple_of(me * own, GROUP), own)

    loads = [
        pltpu.make_async_copy(src, dst, local_sem.at[i])
        for i, (src, dst) in enumerate([(par_hbm, par), (so_hbm, so), (tok_hbm, tok), (go_hbm, go)])
    ]
    for load in loads:
        load.start()

    barrier = pltpu.get_barrier_semaphore()
    for k in range(1, n):
        pl.semaphore_signal(barrier, inc=1, device_id=(mz, flip(me, k, n)), device_id_type=pl.DeviceIdType.MESH)
    for k in range(1, m):
        pl.semaphore_signal(barrier, inc=1, device_id=(flip(mz, k, m), me), device_id_type=pl.DeviceIdType.MESH)
    pl.semaphore_wait(barrier, n + m - 2)

    def to_expert(src, dst, send, recv, k):
        return pltpu.make_async_remote_copy(
            src_ref=src, dst_ref=dst, send_sem=send.at[k], recv_sem=recv.at[k],
            device_id=(mz, flip(me, k, n)), device_id_type=pl.DeviceIdType.MESH,
        )

    def to_dp(src, dst, send, recv, k):
        return pltpu.make_async_remote_copy(
            src_ref=src, dst_ref=dst, send_sem=send.at[k], recv_sem=recv.at[k],
            device_id=(flip(mz, k, m), me), device_id_type=pl.DeviceIdType.MESH,
        )

    loads[0].wait()
    p_copies = [to_expert(par.at[:, my_cols], allp.at[my_rows, my_cols], p_send, p_recv, k) for k in range(1, n)]
    for copy in p_copies:
        copy.start()
    allp[my_rows, my_cols] = par[:, my_cols]

    loads[1].wait()
    out_r = lax.broadcasted_iota(jnp.int32, (imgs * GROUP, GROUP * all_img), 0)
    in_c = lax.broadcasted_iota(jnp.int32, (imgs * GROUP, GROUP * all_img), 1)
    base = in_c - (out_r % GROUP) * all_img - out_r // GROUP

    def relayout(dest, out):
        pick = jnp.where(base == dest * imgs, 1.0, 0.0).astype(BF)

        def one(g, carry):
            s0 = pl.multiple_of(g * GROUP, GROUP)
            block = so[pl.ds(s0, GROUP)].reshape(GROUP * all_img, width)
            moved = jnp.dot(pick, block, preferred_element_type=F32).astype(BF)
            out[:, pl.ds(s0, GROUP), :] = moved.reshape(imgs, GROUP, width)
            return carry

        lax.fori_loop(0, own // GROUP, one, 0)

    order = send_order(n, core)
    a_copies = []
    for k in order:
        relayout(flip(me, k, n), stage.at[k])
        copy = to_expert(stage.at[k], rows.at[me], a_send, a_recv, k)
        copy.start()
        a_copies.append(copy)
    relayout(me, rows.at[me])

    for copy in p_copies:
        copy.wait_recv()
    q_copies = [to_dp(allp.at[:, my_cols], allp.at[:, my_cols], q_send, q_recv, k) for k in range(1, m)]
    for copy in q_copies:
        copy.start()
    loads[2].wait()
    loads[3].wait()
    for copy in q_copies:
        copy.wait_recv()

    def forward(b, carry):
        logits = rows_last(allp[...], tok[b])
        peak = jnp.max(logits, axis=0, keepdims=True)
        raised = jnp.exp(logits - peak)
        weights = raised / jnp.sum(raised, axis=0, keepdims=True)
        comb[b] = weights
        grads = jnp.dot(weights.astype(BF), go[b], preferred_element_type=F32).astype(BF)
        gs[:, b] = grads.reshape(n, own, width)
        return carry

    lax.fori_loop(0, imgs, forward, 0)

    keep = pltpu.make_async_copy(gs.at[me], grec.at[me], local_sem.at[4])
    keep.start()
    g_copies = []
    for k in order:
        copy = to_expert(gs.at[flip(me, k, n)], grec.at[me], g_send, g_recv, k)
        copy.start()
        g_copies.append(copy)

    for copy in a_copies:
        copy.wait_recv()
    acc[...] = jnp.zeros_like(acc)

    def backward(b, carry):
        grad_comb = rows_last(rows[:, b].reshape(slots, width), go[b])
        weights = comb[b]
        rowdot = jnp.sum(weights * grad_comb, axis=0, keepdims=True)
        wide = weights * (grad_comb - rowdot)
        acc[...] += jnp.dot(wide.astype(BF), tok[b], preferred_element_type=F32)
        gt[b] = jnp.dot(wide.T.astype(BF), allp[...], preferred_element_type=F32).astype(BF)
        return carry

    lax.fori_loop(0, imgs, backward, 0)

    for k in range(1, m):
        there = flip(mz, k, m)
        psend[k] = acc[:, pl.ds(pl.multiple_of(there * cols, 128), cols)].astype(BF)
    z_copies = [to_dp(psend.at[k], precv.at[k], z_send, z_recv, k) for k in range(1, m)]
    for copy in z_copies:
        copy.start()
    put = pltpu.make_async_copy(gt, gt_out, local_sem.at[5])
    put.start()
    for copy in z_copies:
        copy.wait_recv()
    total = acc[:, my_cols]
    for k in range(1, m):
        total = total + precv[k].astype(F32)
    acc[:, my_cols] = total
    for k in range(1, n):
        there = flip(me, k, n)
        xsend[k] = acc[pl.ds(pl.multiple_of(there * own, GROUP), own), my_cols].astype(BF)
    x_copies = [to_expert(xsend.at[k], xrecv.at[k], x_send, x_recv, k) for k in range(1, n)]
    for copy in x_copies:
        copy.start()
    for copy in x_copies:
        copy.wait_recv()
    owned = acc[my_rows, my_cols]
    for k in range(1, n):
        owned = owned + xrecv[k].astype(F32)
    gp[...] = owned
    give = pltpu.make_async_copy(gp, gp_out, local_sem.at[6])
    give.start()

    for copy in g_copies:
        copy.wait_recv()
    for copy in p_copies + a_copies + q_copies + g_copies + z_copies + x_copies:
        copy.wait_send()
    keep.wait()
    put.wait()
    give.wait()


def exchange(n, m, tok, go, so, par):
    imgs, patches, width = tok.shape
    own, all_img, _ = so.shape
    slots, cols = own * n, width // m
    dma = pltpu.SemaphoreType.DMA
    return pl.pallas_call(
        functools.partial(exchange_kernel, n, m),
        out_shape=(
            jax.ShapeDtypeStruct((n, imgs, own, width), BF),
            jax.ShapeDtypeStruct((imgs, patches, width), BF),
            jax.ShapeDtypeStruct((own, cols), F32),
        ),
        in_specs=[pl.BlockSpec(memory_space=pl.ANY)] * 4,
        out_specs=(pl.BlockSpec(memory_space=pl.ANY),) * 3,
        scratch_shapes=[
            pltpu.VMEM((imgs, patches, width), BF),
            pltpu.VMEM((imgs, patches, width), BF),
            pltpu.VMEM((own, all_img, width), BF),
            pltpu.VMEM((own, width), BF),
            pltpu.VMEM((slots, width), BF),
            pltpu.VMEM((n, imgs, own, width), BF),
            pltpu.VMEM((n, imgs, own, width), BF),
            pltpu.VMEM((n, imgs, own, width), BF),
            pltpu.VMEM((imgs, slots, patches), F32),
            pltpu.VMEM((imgs, patches, width), BF),
            pltpu.VMEM((slots, width), F32),
            pltpu.VMEM((m, slots, cols), BF),
            pltpu.VMEM((m, slots, cols), BF),
            pltpu.VMEM((n, own, cols), BF),
            pltpu.VMEM((n, own, cols), BF),
            pltpu.VMEM((own, cols), F32),
            dma((7,)),
            dma((n,)), dma((n,)), dma((m,)), dma((m,)),
            dma((n,)), dma((n,)), dma((n,)), dma((n,)),
            dma((m,)), dma((m,)), dma((n,)), dma((n,)),
        ],
        compiler_params=pltpu.CompilerParams(
            collective_id=0, has_side_effects=True, vmem_limit_bytes=66 * 1000 * 1000
        ),
    )(tok, go, so, par)


AXES = ((2, (4, 5, 1)), (4, (2, 3, 1)))


def side_spot(which, index):
    high = index // 4 if which == 0 else (index // 2) % 2
    return high * 2 + index % 2


def paired_kernel(
    n, m, tok_hbm, go_hbm, so_hbm, par_hbm,
    grec, gt_out, gp_out,
    tok, go, mate, so, par, allp, stage, rows, gs, comb, gcf, low, low_send, gc_send, gc_recv,
    gt, acc, ksend, krecv, red, psend, precv, xsend, xrecv, gp,
    local_sem, keep_sem, p_send, p_recv, q_send, q_recv, f_send, f_recv, k_send, k_recv, o_send, o_recv, a_send, a_recv, w_send, w_recv,
    c_send, c_recv, g_send, g_recv, z_send, z_recv, x_send, x_recv,
):
    me = lax.axis_index("expert")
    mz = lax.axis_index("dp")
    imgs = tok.shape[0]
    half = imgs // 2
    own = par.shape[0]
    all_img = so.shape[1]
    slots, width = allp.shape
    patches = tok.shape[1]
    cols = width // m
    quarter = slots // 4
    my_cols = pl.ds(pl.multiple_of(mz * cols, 128), cols)
    my_rows = pl.ds(pl.multiple_of(me * own, GROUP), own)
    sides = ((me // 2) % 2, me // 4)

    def piece(which, other, p):
        side = 1 - sides[which] if other else sides[which]
        start = p * 2 * quarter + side * quarter if which == 0 else side * 2 * quarter + p * quarter
        return pl.ds(pl.multiple_of(start, quarter), quarter)

    loads = [
        pltpu.make_async_copy(src, dst, local_sem.at[i])
        for i, (src, dst) in enumerate([(par_hbm, par), (so_hbm, so), (tok_hbm, tok), (go_hbm, go)])
    ]
    for i in (0, 3, 1, 2):
        loads[i].start()

    barrier = pltpu.get_barrier_semaphore()
    for k in range(1, n):
        pl.semaphore_signal(barrier, inc=1, device_id=(mz, flip(me, k, n)), device_id_type=pl.DeviceIdType.MESH)
    for k in range(1, m):
        pl.semaphore_signal(barrier, inc=1, device_id=(flip(mz, k, m), me), device_id_type=pl.DeviceIdType.MESH)
    pl.semaphore_wait(barrier, n + m - 2)

    def to_expert(src, dst, send, recv, k):
        return pltpu.make_async_remote_copy(
            src_ref=src, dst_ref=dst, send_sem=send, recv_sem=recv,
            device_id=(mz, flip(me, k, n)), device_id_type=pl.DeviceIdType.MESH,
        )

    def to_dp(src, dst, send, recv):
        return [
            pltpu.make_async_remote_copy(
                src_ref=src(k), dst_ref=dst(k), send_sem=send.at[k], recv_sem=recv.at[k],
                device_id=(flip(mz, k, m), me), device_id_type=pl.DeviceIdType.MESH,
            )
            for k in range(1, m)
        ]

    sent = []

    def launch(copies):
        for copy in copies:
            copy.start()
        sent.extend(copies)
        return copies

    def arrive(copies):
        for copy in copies:
            copy.wait_recv()

    loads[0].wait()
    p_copies = launch([
        to_expert(par.at[:, my_cols], allp.at[my_rows, my_cols], p_send.at[k], p_recv.at[k], k)
        for k in range(2, n, 2)
    ])
    allp[my_rows, my_cols] = par[:, my_cols]
    loads[3].wait()
    o_copies = launch([
        to_expert(go.at[pl.ds(q * half, half)], mate.at[q], o_send.at[q], o_recv.at[q], AXES[q][0]) for q in range(2)
    ])

    loads[1].wait()
    out_r = lax.broadcasted_iota(jnp.int32, (imgs * GROUP, GROUP * all_img), 0)
    in_c = lax.broadcasted_iota(jnp.int32, (imgs * GROUP, GROUP * all_img), 1)
    base = in_c - (out_r % GROUP) * all_img - (out_r // GROUP) % half
    first = out_r < half * GROUP

    def relayout(q, dest, out):
        own_at = dest * imgs + q * half
        mate_at = flip(dest, AXES[q][0], n) * imgs + q * half
        pick = jnp.where(base == jnp.where(first, own_at, mate_at), 1.0, 0.0).astype(BF)

        def one(g, carry):
            s0 = pl.multiple_of(g * GROUP, GROUP)
            block = so[pl.ds(s0, GROUP)].reshape(GROUP * all_img, width)
            moved = jnp.dot(pick, block, preferred_element_type=F32).astype(BF)
            out[:, pl.ds(s0, GROUP), :] = moved.reshape(imgs, GROUP, width)
            return carry

        lax.fori_loop(0, own // GROUP, one, 0)

    a_copies = []
    for i in range(3):
        for q in range(2):
            k = AXES[q][1][i]
            relayout(q, flip(me, k, n), stage.at[q, i])
            a_copies += launch([
                to_expert(stage.at[q, i], rows.at[q, side_spot(q, me)], a_send.at[q, i], a_recv.at[q, i], k)
            ])
    for q in range(2):
        relayout(q, me, rows.at[q, side_spot(q, me)])

    arrive(p_copies)
    q_copies = []
    for i in range(n // 2):
        block = allp.at[pl.ds(pl.multiple_of(flip(me, 2 * i, n) * own, GROUP), own), my_cols]
        q_copies += launch(to_dp(lambda k: block, lambda k: block, q_send.at[i], q_recv.at[i]))
    loads[2].wait()
    arrive(q_copies)
    f_copies = []
    for i in range(n // 2):
        block = allp.at[pl.ds(pl.multiple_of(flip(me, 2 * i, n) * own, GROUP), own)]
        f_copies += launch([to_expert(block, block, f_send.at[i], f_recv.at[i], 1)])
    arrive(f_copies)

    w_copies = []
    for q in range(2):

        def forward(t, carry):
            b = q * half + t
            logits = rows_last(allp[...], tok[b])
            peak = jnp.max(logits, axis=0, keepdims=True)
            raised = jnp.exp(logits - peak)
            comb[b] = raised / jnp.sum(raised, axis=0, keepdims=True)
            for p in range(2):
                low[q, t, p * quarter : (p + 1) * quarter] = comb[b, piece(q, False, p)].astype(BF)
                low_send[q, t, p * quarter : (p + 1) * quarter] = comb[b, piece(q, True, p)].astype(BF)
            return carry

        lax.fori_loop(0, half, forward, 0)
        w_copies += launch([
            to_expert(low_send.at[q], low.at[q, pl.ds(half, half)], w_send.at[q], w_recv.at[q], AXES[q][0])
        ])

    def slot_grads(q, i, grads_in):
        out = jnp.dot(low[q, i], grads_in, preferred_element_type=F32).astype(BF)
        gs[q, :, i] = out.reshape(4, own, width)

    def comb_grads(q, i, grads_in):
        return rows_last(rows[q, :, i].reshape(4 * own, width), grads_in)

    for q in range(2):

        def own_slots(t, carry):
            slot_grads(q, t, go[q * half + t])
            return carry

        lax.fori_loop(0, half, own_slots, 0)

    arrive(o_copies)
    arrive(a_copies)
    c_copies = []
    for q in range(2):

        def mate_comb(t, carry):
            gc_send[q, t] = comb_grads(q, half + t, mate[q, t]).astype(BF)
            return carry

        lax.fori_loop(0, half, mate_comb, 0)
        c_copies += launch([to_expert(gc_send.at[q], gc_recv.at[q], c_send.at[q], c_recv.at[q], AXES[q][0])])

    keeps = []

    def return_grads(h):
        copies = []
        for i in range(3):
            for q in range(2):
                k = AXES[q][1][i]
                holder = flip(me, AXES[q][0], n) if h else me
                part, images = pl.ds(h * half, half), pl.ds(q * half, half)
                copies += launch([
                    to_expert(
                        gs.at[q, side_spot(q, flip(me, k, n)), part], grec.at[holder, images],
                        g_send.at[h, q, i], g_recv.at[h, q, i], k,
                    )
                ])
        for q in range(2):
            holder = flip(me, AXES[q][0], n) if h else me
            keep = pltpu.make_async_copy(
                gs.at[q, side_spot(q, me), pl.ds(h * half, half)],
                grec.at[holder, pl.ds(q * half, half)], keep_sem.at[h, q],
            )
            keep.start()
            keeps.append(keep)
        return copies

    g_copies = return_grads(0)
    arrive(w_copies)
    for q in range(2):

        def mate_slots(t, carry):
            slot_grads(q, half + t, mate[q, t])
            return carry

        lax.fori_loop(0, half, mate_slots, 0)
    g_copies += return_grads(1)

    for q in range(2):

        def own_comb(t, carry):
            grads = comb_grads(q, t, go[q * half + t])
            for p in range(2):
                gcf[q * half + t, piece(q, False, p)] = grads[p * quarter : (p + 1) * quarter]
            return carry

        lax.fori_loop(0, half, own_comb, 0)
    acc[...] = jnp.zeros_like(acc)
    arrive(c_copies)
    for q in range(2):

        def backward(t, carry):
            b = q * half + t
            for p in range(2):
                gcf[b, piece(q, True, p)] = gc_recv[q, t, p * quarter : (p + 1) * quarter].astype(F32)
            grad_comb = gcf[b]
            weights = comb[b]
            rowdot = jnp.sum(weights * grad_comb, axis=0, keepdims=True)
            wide = weights * (grad_comb - rowdot)
            gcf[b] = wide
            acc[...] += jnp.dot(wide.astype(BF), tok[b], preferred_element_type=F32)
            return carry

        lax.fori_loop(0, half, backward, 0)

    core = me % 2
    for i in range(n // 2):
        ksend[i] = acc[pl.ds(pl.multiple_of((2 * i + 1 - core) * own, GROUP), own)].astype(BF)
    k_copies = launch([to_expert(ksend, krecv, k_send.at[0], k_recv.at[0], 1)])
    arrive(k_copies)
    for i in range(n // 2):
        red[i] = acc[pl.ds(pl.multiple_of((2 * i + core) * own, GROUP), own)] + krecv[i].astype(F32)
    for k in range(1, m):
        there = flip(mz, k, m)
        psend[k] = red[:, :, pl.ds(pl.multiple_of(there * cols, 128), cols)].astype(BF)
    z_copies = launch(to_dp(lambda k: psend.at[k], lambda k: precv.at[k], z_send, z_recv))

    def token_grads(b, carry):
        gt[b] = jnp.dot(gcf[b].T.astype(BF), allp[...], preferred_element_type=F32).astype(BF)
        return carry

    lax.fori_loop(0, imgs, token_grads, 0)
    put = pltpu.make_async_copy(gt, gt_out, local_sem.at[5])
    put.start()
    arrive(z_copies)
    total = red[:, :, my_cols]
    for k in range(1, m):
        total = total + precv[k].astype(F32)
    red[:, :, my_cols] = total
    for k in range(2, n, 2):
        xsend[k // 2] = red[flip(me, k, n) // 2, :, my_cols].astype(BF)
    x_copies = launch([
        to_expert(xsend.at[k // 2], xrecv.at[k // 2], x_send.at[k], x_recv.at[k], k) for k in range(2, n, 2)
    ])
    arrive(x_copies)
    owned = red[me // 2, :, my_cols]
    for k in range(2, n, 2):
        owned = owned + xrecv[k // 2].astype(F32)
    gp[...] = owned
    give = pltpu.make_async_copy(gp, gp_out, local_sem.at[6])
    give.start()

    arrive(g_copies)
    for copy in sent:
        copy.wait_send()
    for keep in keeps:
        keep.wait()
    put.wait()
    give.wait()


def paired_exchange(n, m, tok, go, so, par):
    imgs, patches, width = tok.shape
    own, all_img, _ = so.shape
    slots, cols, half = own * n, width // m, imgs // 2
    dma = pltpu.SemaphoreType.DMA
    return pl.pallas_call(
        functools.partial(paired_kernel, n, m),
        out_shape=(
            jax.ShapeDtypeStruct((n, imgs, own, width), BF),
            jax.ShapeDtypeStruct((imgs, patches, width), BF),
            jax.ShapeDtypeStruct((own, cols), F32),
        ),
        in_specs=[pl.BlockSpec(memory_space=pl.ANY)] * 4,
        out_specs=(pl.BlockSpec(memory_space=pl.ANY),) * 3,
        scratch_shapes=[
            pltpu.VMEM((imgs, patches, width), BF),
            pltpu.VMEM((imgs, patches, width), BF),
            pltpu.VMEM((2, half, patches, width), BF),
            pltpu.VMEM((own, all_img, width), BF),
            pltpu.VMEM((own, width), BF),
            pltpu.VMEM((slots, width), BF),
            pltpu.VMEM((2, 3, imgs, own, width), BF),
            pltpu.VMEM((2, 4, imgs, own, width), BF),
            pltpu.VMEM((2, 4, imgs, own, width), BF),
            pltpu.VMEM((imgs, slots, patches), F32),
            pltpu.VMEM((imgs, slots, patches), F32),
            pltpu.VMEM((2, imgs, slots // 2, patches), BF),
            pltpu.VMEM((2, half, slots // 2, patches), BF),
            pltpu.VMEM((2, half, slots // 2, patches), BF),
            pltpu.VMEM((2, half, slots // 2, patches), BF),
            pltpu.VMEM((imgs, patches, width), BF),
            pltpu.VMEM((slots, width), F32),
            pltpu.VMEM((n // 2, own, width), BF),
            pltpu.VMEM((n // 2, own, width), BF),
            pltpu.VMEM((n // 2, own, width), F32),
            pltpu.VMEM((m, n // 2, own, cols), BF),
            pltpu.VMEM((m, n // 2, own, cols), BF),
            pltpu.VMEM((n // 2, own, cols), BF),
            pltpu.VMEM((n // 2, own, cols), BF),
            pltpu.VMEM((own, cols), F32),
            dma((7,)), dma((2, 2)),
            dma((n,)), dma((n,)), dma((n // 2, m)), dma((n // 2, m)),
            dma((n // 2,)), dma((n // 2,)), dma((1,)), dma((1,)),
            dma((2,)), dma((2,)), dma((2, 3)), dma((2, 3)), dma((2,)), dma((2,)),
            dma((2,)), dma((2,)), dma((2, 2, 3)), dma((2, 2, 3)),
            dma((m,)), dma((m,)), dma((n,)), dma((n,)),
        ],
        compiler_params=pltpu.CompilerParams(
            collective_id=0, has_side_effects=True, vmem_limit_bytes=66 * 1000 * 1000
        ),
    )(tok, go, so, par)


def settle_kernel(arrived, gp_in, out, gp_out):
    out[...] = jnp.swapaxes(arrived[...], 0, 1)
    gp_out[...] = gp_in[...]


def settle(arrived, grad_par):
    all_img, own, width = arrived.shape
    small = pl.BlockSpec((GROUP, grad_par.shape[1]), lambda i: (i, 0))
    return pl.pallas_call(
        settle_kernel,
        grid=(own // GROUP,),
        out_shape=(
            jax.ShapeDtypeStruct((own, all_img, width), BF),
            jax.ShapeDtypeStruct(grad_par.shape, F32),
        ),
        in_specs=[pl.BlockSpec((all_img, GROUP, width), lambda i: (0, i, 0)), small],
        out_specs=(pl.BlockSpec((GROUP, all_img, width), lambda i: (i, 0, 0)), small),
    )(arrived, grad_par)


def per_device(n, m, tokens, grad_out, slot_out, slot_params):
    tok = jnp.transpose(tokens, (1, 0, 2))
    go = jnp.transpose(grad_out, (1, 0, 2))
    plan = paired_exchange if n == 8 and tok.shape[0] % 2 == 0 else exchange
    arrived, grad_tok, grad_par = plan(n, m, tok, go, slot_out, slot_params)
    own, all_img, width = slot_out.shape
    grad_slot, grad_par = settle(arrived.reshape(all_img, own, width), grad_par)
    return jnp.transpose(grad_tok, (1, 0, 2)), grad_slot, grad_par


def solution(mesh):
    return jax.shard_map(
        functools.partial(per_device, mesh.shape["expert"], mesh.shape["dp"]),
        mesh=mesh,
        in_specs=(
            P(None, ("dp", "expert"), None),
            P(None, ("dp", "expert"), None),
            P("expert", "dp", None),
            P("expert", None),
        ),
        out_specs=(P(None, ("dp", "expert"), None), P("expert", "dp", None), P("expert", "dp")),
        check_vma=False,
    )
```

profile of v0, /device:TPU:0, one launch (start us, length us, event | category | flops | bytes accessed | tf_op | source)
XLA Modules:
  0.0 139.7 jit_solution(10817677100961227470)
XLA Ops:
  0.6 130.7 %shard_map.67 = (bf16[8,6,64,1024]{3,2,1,0:T(8,128)(2,1)}, bf16[6,256,1024]{2,1,0:T(8,128)(2,1)}, f32[64,256]{1,0:T(8,128)}) custom-call(bf16[6,256,1024]{2,1,0:T(8,128)(2,1)} %bitcast.6, bf16[6,256,1024]{2,1,0:T(8,128)(2,1)} %bitcast.7, bf16[64,48,1024]{2,1,0:T(8,128)(2,1)} %so_hbm.1, bf16[64,1024]{1,0:T(8,128)(2,1)} %par_hbm.1), custom_call_target="tpu_custom_call" | custom-call | tf_op jit(solution)/shard_map/pallas_call | solution.py:529
  131.4 0.0 copy-start
  131.4 6.7 %shard_map.68 = (bf16[64,48,1024]{2,1,0:T(8,128)(2,1)}, f32[64,256]{1,0:T(8,128)}) custom-call(bf16[48,64,1024]{2,1,0:T(8,128)(2,1)} %bitcast.4, f32[64,256]{1,0:T(8,128)} %get-tuple-element.10.gp_in), custom_call_target="tpu_custom_call" | custom-call | tf_op jit(solution)/shard_map/pallas_call | solution.py:585
  138.1 0.0 copy-done
  138.1 1.7 %copy.8 = bf16[256,6,1024]{2,0,1:T(8,128)(2,1)} copy(bf16[256,6,1024]{2,0,1:T(8,128)(2,1)S(1)} %bitcast.5) | data formatting | bytes 6291456
Async XLA Ops:
  131.4 6.7 %copy-start = (bf16[6,256,1024]{2,1,0:T(8,128)(2,1)S(1)}, bf16[6,256,1024]{2,1,0:T(8,128)(2,1)}, u32[]{:S(2)}) copy-start(bf16[6,256,1024]{2,1,0:T(8,128)(2,1)} %get-tuple-element.8) | copy-start | bytes 9437188
where the time goes:
time: 140 us
  Pallas kernels  137 us (98%)
  local copies, waits for them, and re-layouts  1.67 us (1%)
    pallas_call x1, Pallas kernels, paired_exchange(): pl.pallas_call(functools.partial(paired_kernel, n, m), out_shape=(jax.Sha...  131 us
    pallas_call x1, Pallas kernels, settle(): pl.pallas_call(settle_kernel, grid=(own // GROUP,), out_shape=(jax.ShapeD...  6.68 us

commit v1 on v0

--- a/solution.py
+++ b/solution.py
@@ -10,6 +10,7 @@
 BF = jnp.bfloat16
 F32 = jnp.float32
 GROUP = 16
+LANES = 128
 
 
 def flip(index, mask, size):
@@ -245,9 +246,9 @@
 
 def paired_kernel(
     n, m, tok_hbm, go_hbm, so_hbm, par_hbm,
-    grec, gt_out, gp_out,
+    done, last, gt, gp,
     tok, go, mate, so, par, allp, stage, rows, gs, comb, gcf, low, low_send, gc_send, gc_recv,
-    gt, acc, ksend, krecv, red, psend, precv, xsend, xrecv, gp,
+    grec, acc, ksend, krecv, red, psend, precv, xsend, xrecv,
     local_sem, keep_sem, p_send, p_recv, q_send, q_recv, f_send, f_recv, k_send, k_recv, o_send, o_recv, a_send, a_recv, w_send, w_recv,
     c_send, c_recv, g_send, g_recv, z_send, z_recv, x_send, x_recv,
 ):
@@ -412,32 +413,39 @@
         lax.fori_loop(0, half, mate_comb, 0)
         c_copies += launch([to_expert(gc_send.at[q], gc_recv.at[q], c_send.at[q], c_recv.at[q], AXES[q][0])])
 
+    chunks = own // GROUP
     keeps = []
 
-    def return_grads(h):
-        copies = []
-        for i in range(3):
+    def landing(holder, images, j):
+        if j == chunks - 1:
+            return last.at[holder, images]
+        return grec.at[holder, images, pl.ds(j * GROUP, GROUP)]
+
+    def return_grads(h, parts):
+        part = pl.ds(h * half, half)
+        for j in parts:
+            for i in range(3):
+                for q in range(2):
+                    k = AXES[q][1][i]
+                    holder = flip(me, AXES[q][0], n) if h else me
+                    to_expert(
+                        gs.at[q, side_spot(q, flip(me, k, n)), part, pl.ds(j * GROUP, GROUP)],
+                        landing(holder, pl.ds(q * half, half), j), g_send.at[j], g_recv.at[j], k,
+                    ).start()
             for q in range(2):
-                k = AXES[q][1][i]
                 holder = flip(me, AXES[q][0], n) if h else me
-                part, images = pl.ds(h * half, half), pl.ds(q * half, half)
-                copies += launch([
-                    to_expert(
-                        gs.at[q, side_spot(q, flip(me, k, n)), part], grec.at[holder, images],
-                        g_send.at[h, q, i], g_recv.at[h, q, i], k,
-                    )
-                ])
-        for q in range(2):
-            holder = flip(me, AXES[q][0], n) if h else me
-            keep = pltpu.make_async_copy(
-                gs.at[q, side_spot(q, me), pl.ds(h * half, half)],
-                grec.at[holder, pl.ds(q * half, half)], keep_sem.at[h, q],
-            )
-            keep.start()
-            keeps.append(keep)
-        return copies
-
-    g_copies = return_grads(0)
+                keep = pltpu.make_async_copy(
+                    gs.at[q, side_spot(q, me), part, pl.ds(j * GROUP, GROUP)],
+                    landing(holder, pl.ds(q * half, half), j), keep_sem.at[h, q, j],
+                )
+                keep.start()
+                keeps.append(keep)
+
+    def grads_moved(j):
+        every = last.at[: n - 2] if j == chunks - 1 else grec.at[: n - 2, :, pl.ds(j * GROUP, GROUP)]
+        return to_expert(every, every, g_send.at[j], g_recv.at[j], 1)
+
+    return_grads(0, range(chunks))
     arrive(w_copies)
     for q in range(2):
 
@@ -446,7 +454,7 @@
             return carry
 
         lax.fori_loop(0, half, mate_slots, 0)
-    g_copies += return_grads(1)
+    return_grads(1, range(chunks - 1))
 
     for q in range(2):
 
@@ -492,8 +500,6 @@
         return carry
 
     lax.fori_loop(0, imgs, token_grads, 0)
-    put = pltpu.make_async_copy(gt, gt_out, local_sem.at[5])
-    put.start()
     arrive(z_copies)
     total = red[:, :, my_cols]
     for k in range(1, m):
@@ -504,21 +510,29 @@
     x_copies = launch([
         to_expert(xsend.at[k // 2], xrecv.at[k // 2], x_send.at[k], x_recv.at[k], k) for k in range(2, n, 2)
     ])
+    return_grads(1, (chunks - 1,))
+    for keep in keeps:
+        keep.wait()
+    for j in range(chunks - 1):
+        grads_moved(j).wait_recv()
+
+        def swap(c, carry):
+            lanes = pl.ds(pl.multiple_of(c * LANES, LANES), LANES)
+            block = grec[:, :, j * GROUP : (j + 1) * GROUP, lanes].reshape(n * imgs, GROUP, LANES)
+            done[j * GROUP : (j + 1) * GROUP, :, lanes] = jnp.swapaxes(block, 0, 1)
+            return carry
+
+        lax.fori_loop(0, width // LANES, swap, 0)
     arrive(x_copies)
     owned = red[me // 2, :, my_cols]
     for k in range(2, n, 2):
         owned = owned + xrecv[k // 2].astype(F32)
     gp[...] = owned
-    give = pltpu.make_async_copy(gp, gp_out, local_sem.at[6])
-    give.start()
-
-    arrive(g_copies)
     for copy in sent:
         copy.wait_send()
-    for keep in keeps:
-        keep.wait()
-    put.wait()
-    give.wait()
+    for j in range(chunks):
+        grads_moved(j).wait_send()
+    grads_moved(chunks - 1).wait_recv()
 
 
 def paired_exchange(n, m, tok, go, so, par):
@@ -529,12 +543,13 @@
     return pl.pallas_call(
         functools.partial(paired_kernel, n, m),
         out_shape=(
-            jax.ShapeDtypeStruct((n, imgs, own, width), BF),
-            jax.ShapeDtypeStruct((imgs, patches, width), BF),
-            jax.ShapeDtypeStruct((own, cols), F32),
+            pltpu.VMEM((own - GROUP, all_img, width), BF),
+            pltpu.VMEM((n, imgs, GROUP, width), BF),
+            pltpu.VMEM((imgs, patches, width), BF),
+            pltpu.VMEM((own, cols), F32),
         ),
         in_specs=[pl.BlockSpec(memory_space=pl.ANY)] * 4,
-        out_specs=(pl.BlockSpec(memory_space=pl.ANY),) * 3,
+        out_specs=(pl.BlockSpec(memory_space=pltpu.VMEM),) * 4,
         scratch_shapes=[
             pltpu.VMEM((imgs, patches, width), BF),
             pltpu.VMEM((imgs, patches, width), BF),
@@ -551,7 +566,7 @@
             pltpu.VMEM((2, half, slots // 2, patches), BF),
             pltpu.VMEM((2, half, slots // 2, patches), BF),
             pltpu.VMEM((2, half, slots // 2, patches), BF),
-            pltpu.VMEM((imgs, patches, width), BF),
+            pltpu.VMEM((n, imgs, own - GROUP, width), BF),
             pltpu.VMEM((slots, width), F32),
             pltpu.VMEM((n // 2, own, width), BF),
             pltpu.VMEM((n // 2, own, width), BF),
@@ -560,16 +575,15 @@
             pltpu.VMEM((m, n // 2, own, cols), BF),
             pltpu.VMEM((n // 2, own, cols), BF),
             pltpu.VMEM((n // 2, own, cols), BF),
-            pltpu.VMEM((own, cols), F32),
-            dma((7,)), dma((2, 2)),
+            dma((4,)), dma((2, 2, own // GROUP)),
             dma((n,)), dma((n,)), dma((n // 2, m)), dma((n // 2, m)),
             dma((n // 2,)), dma((n // 2,)), dma((1,)), dma((1,)),
             dma((2,)), dma((2,)), dma((2, 3)), dma((2, 3)), dma((2,)), dma((2,)),
-            dma((2,)), dma((2,)), dma((2, 2, 3)), dma((2, 2, 3)),
+            dma((2,)), dma((2,)), dma((own // GROUP,)), dma((own // GROUP,)),
             dma((m,)), dma((m,)), dma((n,)), dma((n,)),
         ],
         compiler_params=pltpu.CompilerParams(
-            collective_id=0, has_side_effects=True, vmem_limit_bytes=66 * 1000 * 1000
+            collective_id=0, has_side_effects=True, vmem_limit_bytes=56 * 1000 * 1000
         ),
     )(tok, go, so, par)
 
@@ -594,13 +608,54 @@
     )(arrived, grad_par)
 
 
+def finish_kernel(done, last, gt, gp, slot_out, tok_out, par_out, turned, sem):
+    own = done.shape[0]
+    copies = [
+        pltpu.make_async_copy(done, slot_out.at[pl.ds(0, own)], sem.at[0]),
+        pltpu.make_async_copy(gt, tok_out, sem.at[1]),
+        pltpu.make_async_copy(gp, par_out, sem.at[2]),
+    ]
+    for copy in copies:
+        copy.start()
+    group, all_img, width = turned.shape
+
+    def swap(c, carry):
+        lanes = pl.ds(pl.multiple_of(c * LANES, LANES), LANES)
+        turned[:, :, lanes] = jnp.swapaxes(last[:, :, :, lanes].reshape(all_img, group, LANES), 0, 1)
+        return carry
+
+    lax.fori_loop(0, width // LANES, swap, 0)
+    copies.append(pltpu.make_async_copy(turned, slot_out.at[pl.ds(own, group)], sem.at[3]))
+    copies[3].start()
+    for copy in copies:
+        copy.wait()
+
+
+def finish(done, last, gt, gp):
+    own, all_img, width = done.shape
+    return pl.pallas_call(
+        finish_kernel,
+        out_shape=(
+            jax.ShapeDtypeStruct((own + GROUP, all_img, width), BF),
+            jax.ShapeDtypeStruct(gt.shape, BF),
+            jax.ShapeDtypeStruct(gp.shape, F32),
+        ),
+        in_specs=[pl.BlockSpec(memory_space=pltpu.VMEM)] * 4,
+        out_specs=(pl.BlockSpec(memory_space=pl.ANY),) * 3,
+        scratch_shapes=[pltpu.VMEM((GROUP, all_img, width), BF), pltpu.SemaphoreType.DMA((4,))],
+        compiler_params=pltpu.CompilerParams(vmem_limit_bytes=16 * 1000 * 1000),
+    )(done, last, gt, gp)
+
+
 def per_device(n, m, tokens, grad_out, slot_out, slot_params):
     tok = jnp.transpose(tokens, (1, 0, 2))
     go = jnp.transpose(grad_out, (1, 0, 2))
-    plan = paired_exchange if n == 8 and tok.shape[0] % 2 == 0 else exchange
-    arrived, grad_tok, grad_par = plan(n, m, tok, go, slot_out, slot_params)
-    own, all_img, width = slot_out.shape
-    grad_slot, grad_par = settle(arrived.reshape(all_img, own, width), grad_par)
+    if n == 8 and tok.shape[0] % 2 == 0:
+        grad_slot, grad_tok, grad_par = finish(*paired_exchange(n, m, tok, go, slot_out, slot_params))
+    else:
+        arrived, grad_tok, grad_par = exchange(n, m, tok, go, slot_out, slot_params)
+        own, all_img, width = slot_out.shape
+        grad_slot, grad_par = settle(arrived.reshape(all_img, own, width), grad_par)
     return jnp.transpose(grad_tok, (1, 0, 2)), grad_slot, grad_par
 
 

time: 140 us -> 133 us (0.950)
  Pallas kernels: 137 us -> 132 us
  local copies, waits for them, and re-layouts: 1.67 us -> 0 us
    pallas_call x2, Pallas kernels: 137 us -> 132 us  [the longest x1 128 us: paired_exchange(): pl.pallas_call(functools.partial(paired_kernel, n, m), out_shape=(pltpu.V...]
    unnamed x3 -> x0, local copies, waits for them, and re-layouts: 1.67 us -> none
where the time goes in v1:
time: 133 us; the launch traced here: 132 us
  Pallas kernels  132 us (99%)
    pallas_call x1, Pallas kernels, paired_exchange(): pl.pallas_call(functools.partial(paired_kernel, n, m), out_shape=(pltpu.V...  128 us
    pallas_call x1, Pallas kernels, finish(): pl.pallas_call(finish_kernel, out_shape=(jax.ShapeDtypeStruct((own + GROU...  3.7 us

profile of v1, /device:TPU:0, one launch (start us, length us, event | category | flops | bytes accessed | tf_op | source)
XLA Modules:
  0.0 132.4 jit_solution(11241049702835290872)
XLA Ops:
  0.6 128.1 %shard_map.67 = (bf16[48,48,1024]{2,1,0:T(8,128)(2,1)S(1)}, bf16[8,6,16,1024]{3,2,1,0:T(8,128)(2,1)S(1)}, bf16[6,256,1024]{2,1,0:T(8,128)(2,1)S(1)}, f32[64,256]{1,0:T(8,128)S(1)}) custom-call(bf16[6,256,1024]{2,1,0:T(8,128)(2,1)} %bitcast.3, bf16[6,256,1024]{2,1,0:T(8,128)(2,1)} %bitcast.4, bf16[64,48,1024]{2,1,0:T(8,128)(2,1)} %so_hbm.1, ...), custom_call_target="tpu_custom_call" | custom-call | tf_op jit(solution)/shard_map/pallas_call | solution.py:543
  128.7 3.7 %shard_map.68 = (bf16[64,48,1024]{2,1,0:T(8,128)(2,1)}, bf16[6,256,1024]{2,1,0:T(8,128)(2,1)}, f32[64,256]{1,0:T(8,128)}) custom-call(bf16[48,48,1024]{2,1,0:T(8,128)(2,1)S(1)} %get-tuple-element.10.done, bf16[8,6,16,1024]{3,2,1,0:T(8,128)(2,1)S(1)} %get-tuple-element.11.last, bf16[6,256,1024]{2,1,0:T(8,128)(2,1)S(1)} %get-tuple-element.12.gt, ...), custom_call_target="tpu_custom_call" | custom-call | tf_op jit(solution)/shard_map/pallas_call | solution.py:636

commit v2 on v1

--- a/solution.py
+++ b/solution.py
@@ -236,6 +236,7 @@
     )(tok, go, so, par)
 
 
+NEAR = (1, 2, 3, 4, 5)
 AXES = ((2, (4, 5, 1)), (4, (2, 3, 1)))
 
 
@@ -249,8 +250,8 @@
     done, last, gt, gp,
     tok, go, mate, so, par, allp, stage, rows, gs, comb, gcf, low, low_send, gc_send, gc_recv,
     grec, acc, ksend, krecv, red, psend, precv, xsend, xrecv,
-    local_sem, keep_sem, p_send, p_recv, q_send, q_recv, f_send, f_recv, k_send, k_recv, o_send, o_recv, a_send, a_recv, w_send, w_recv,
-    c_send, c_recv, g_send, g_recv, z_send, z_recv, x_send, x_recv,
+    ready, corner, local_sem, keep_sem, p_sems, q_sems, f_sems, k_sems, o_sems, a_sems, w_sems,
+    c_sems, g_sems, z_sems, x_sems,
 ):
     me = lax.axis_index("expert")
     mz = lax.axis_index("dp")
@@ -278,12 +279,50 @@
     for i in (0, 3, 1, 2):
         loads[i].start()
 
+    gate = n - 1
     barrier = pltpu.get_barrier_semaphore()
-    for k in range(1, n):
-        pl.semaphore_signal(barrier, inc=1, device_id=(mz, flip(me, k, n)), device_id_type=pl.DeviceIdType.MESH)
-    for k in range(1, m):
-        pl.semaphore_signal(barrier, inc=1, device_id=(flip(mz, k, m), me), device_id_type=pl.DeviceIdType.MESH)
-    pl.semaphore_wait(barrier, n + m - 2)
+
+    def tell(sem, plane, index):
+        pl.semaphore_signal(sem, inc=1, device_id=(plane, index), device_id_type=pl.DeviceIdType.MESH)
+
+    for k in NEAR:
+
+        @pl.when(flip(me, k, n) != gate)
+        def greet():
+            tell(barrier, mz, flip(me, k, n))
+
+    @pl.when(me != gate)
+    def meet():
+        pl.semaphore_wait(barrier, len(NEAR))
+
+    @pl.when(me == gate - 1)
+    def admit():
+        tell(ready, mz, gate)
+
+    @pl.when(me == gate)
+    def enter():
+        pl.semaphore_wait(ready, 1)
+
+    tell(corner, mz, flip(me, 2, n))
+
+    def meet_corner():
+        pl.semaphore_wait(corner, 1)
+
+        @pl.when(me == gate)
+        def announce():
+            for k in range(1, m):
+                tell(barrier, flip(mz, k, m), gate)
+
+    def meet_planes():
+        @pl.when(me == gate)
+        def spread():
+            pl.semaphore_wait(barrier, m - 1)
+            for k in range(1, n):
+                tell(ready, mz, flip(me, k, n))
+
+        @pl.when(me != gate)
+        def follow():
+            pl.semaphore_wait(ready, 1)
 
     def to_expert(src, dst, send, recv, k):
         return pltpu.make_async_remote_copy(
@@ -291,37 +330,39 @@
             device_id=(mz, flip(me, k, n)), device_id_type=pl.DeviceIdType.MESH,
         )
 
-    def to_dp(src, dst, send, recv):
-        return [
+    def to_dp(src, dst, sems):
+        for k in range(1, m):
             pltpu.make_async_remote_copy(
-                src_ref=src(k), dst_ref=dst(k), send_sem=send.at[k], recv_sem=recv.at[k],
+                src_ref=src(k), dst_ref=dst(k), send_sem=sems.at[0], recv_sem=sems.at[1],
                 device_id=(flip(mz, k, m), me), device_id_type=pl.DeviceIdType.MESH,
-            )
-            for k in range(1, m)
-        ]
-
-    sent = []
-
-    def launch(copies):
-        for copy in copies:
-            copy.start()
-        sent.extend(copies)
-        return copies
-
-    def arrive(copies):
-        for copy in copies:
-            copy.wait_recv()
+            ).start()
+
+    def send(src, dst, sems, k):
+        to_expert(src, dst, sems.at[0], sems.at[1], k).start()
+
+    groups = []
+
+    def group(every, sems):
+        groups.append(to_expert(every, every, sems.at[0], sems.at[1], 1))
+        return groups[-1]
+
+    def arrive(moved):
+        moved.wait_recv()
 
     loads[0].wait()
-    p_copies = launch([
-        to_expert(par.at[:, my_cols], allp.at[my_rows, my_cols], p_send.at[k], p_recv.at[k], k)
-        for k in range(2, n, 2)
-    ])
+    def send_params(peers):
+        for k in peers:
+            send(par.at[:, my_cols], allp.at[my_rows, my_cols], p_sems, k)
+
+    send_params((2, 4))
+    loads[3].wait()
+    for q in range(2):
+        send(go.at[pl.ds(q * half, half)], mate.at[q], o_sems, AXES[q][0])
+    o_moved = group(mate, o_sems)
+    meet_corner()
+    send_params((6,))
+    p_moved = group(allp.at[pl.ds(0, 3 * own), my_cols], p_sems)
     allp[my_rows, my_cols] = par[:, my_cols]
-    loads[3].wait()
-    o_copies = launch([
-        to_expert(go.at[pl.ds(q * half, half)], mate.at[q], o_send.at[q], o_recv.at[q], AXES[q][0]) for q in range(2)
-    ])
 
     loads[1].wait()
     out_r = lax.broadcasted_iota(jnp.int32, (imgs * GROUP, GROUP * all_img), 0)
@@ -343,31 +384,30 @@
 
         lax.fori_loop(0, own // GROUP, one, 0)
 
-    a_copies = []
     for i in range(3):
         for q in range(2):
             k = AXES[q][1][i]
             relayout(q, flip(me, k, n), stage.at[q, i])
-            a_copies += launch([
-                to_expert(stage.at[q, i], rows.at[q, side_spot(q, me)], a_send.at[q, i], a_recv.at[q, i], k)
-            ])
+            send(stage.at[q, i], rows.at[q, side_spot(q, me)], a_sems, k)
+    a_moved = group(stage, a_sems)
     for q in range(2):
         relayout(q, me, rows.at[q, side_spot(q, me)])
 
-    arrive(p_copies)
-    q_copies = []
+    arrive(p_moved)
+    meet_planes()
     for i in range(n // 2):
         block = allp.at[pl.ds(pl.multiple_of(flip(me, 2 * i, n) * own, GROUP), own), my_cols]
-        q_copies += launch(to_dp(lambda k: block, lambda k: block, q_send.at[i], q_recv.at[i]))
+        to_dp(lambda k: block, lambda k: block, q_sems.at[i])
+    q_moved = [group(precv.at[pl.ds(1, m - 1), 0], q_sems.at[i]) for i in range(n // 2)]
     loads[2].wait()
-    arrive(q_copies)
-    f_copies = []
+    for moved in q_moved:
+        arrive(moved)
     for i in range(n // 2):
         block = allp.at[pl.ds(pl.multiple_of(flip(me, 2 * i, n) * own, GROUP), own)]
-        f_copies += launch([to_expert(block, block, f_send.at[i], f_recv.at[i], 1)])
-    arrive(f_copies)
-
-    w_copies = []
+        send(block, block, f_sems, 1)
+    f_moved = group(allp.at[pl.ds(0, n // 2 * own)], f_sems)
+    arrive(f_moved)
+
     for q in range(2):
 
         def forward(t, carry):
@@ -382,9 +422,8 @@
             return carry
 
         lax.fori_loop(0, half, forward, 0)
-        w_copies += launch([
-            to_expert(low_send.at[q], low.at[q, pl.ds(half, half)], w_send.at[q], w_recv.at[q], AXES[q][0])
-        ])
+        send(low_send.at[q], low.at[q, pl.ds(half, half)], w_sems, AXES[q][0])
+    w_moved = group(low_send, w_sems)
 
     def slot_grads(q, i, grads_in):
         out = jnp.dot(low[q, i], grads_in, preferred_element_type=F32).astype(BF)
@@ -401,9 +440,8 @@
 
         lax.fori_loop(0, half, own_slots, 0)
 
-    arrive(o_copies)
-    arrive(a_copies)
-    c_copies = []
+    arrive(o_moved)
+    arrive(a_moved)
     for q in range(2):
 
         def mate_comb(t, carry):
@@ -411,10 +449,10 @@
             return carry
 
         lax.fori_loop(0, half, mate_comb, 0)
-        c_copies += launch([to_expert(gc_send.at[q], gc_recv.at[q], c_send.at[q], c_recv.at[q], AXES[q][0])])
+        send(gc_send.at[q], gc_recv.at[q], c_sems, AXES[q][0])
+    c_moved = group(gc_send, c_sems)
 
     chunks = own // GROUP
-    keeps = []
 
     def landing(holder, images, j):
         if j == chunks - 1:
@@ -428,25 +466,24 @@
                 for q in range(2):
                     k = AXES[q][1][i]
                     holder = flip(me, AXES[q][0], n) if h else me
-                    to_expert(
+                    send(
                         gs.at[q, side_spot(q, flip(me, k, n)), part, pl.ds(j * GROUP, GROUP)],
-                        landing(holder, pl.ds(q * half, half), j), g_send.at[j], g_recv.at[j], k,
-                    ).start()
+                        landing(holder, pl.ds(q * half, half), j), g_sems.at[j], k,
+                    )
             for q in range(2):
                 holder = flip(me, AXES[q][0], n) if h else me
-                keep = pltpu.make_async_copy(
+                pltpu.make_async_copy(
                     gs.at[q, side_spot(q, me), part, pl.ds(j * GROUP, GROUP)],
-                    landing(holder, pl.ds(q * half, half), j), keep_sem.at[h, q, j],
-                )
-                keep.start()
-                keeps.append(keep)
-
-    def grads_moved(j):
-        every = last.at[: n - 2] if j == chunks - 1 else grec.at[: n - 2, :, pl.ds(j * GROUP, GROUP)]
-        return to_expert(every, every, g_send.at[j], g_recv.at[j], 1)
+                    landing(holder, pl.ds(q * half, half), j), keep_sem.at[j],
+                ).start()
+
+    def all_grads(j, holders):
+        return last.at[:holders] if j == chunks - 1 else grec.at[:holders, :, pl.ds(j * GROUP, GROUP)]
+
+    g_moved = [group(all_grads(j, n - 2), g_sems.at[j]) for j in range(chunks)]
 
     return_grads(0, range(chunks))
-    arrive(w_copies)
+    arrive(w_moved)
     for q in range(2):
 
         def mate_slots(t, carry):
@@ -466,7 +503,7 @@
 
         lax.fori_loop(0, half, own_comb, 0)
     acc[...] = jnp.zeros_like(acc)
-    arrive(c_copies)
+    arrive(c_moved)
     for q in range(2):
 
         def backward(t, carry):
@@ -486,35 +523,38 @@
     core = me % 2
     for i in range(n // 2):
         ksend[i] = acc[pl.ds(pl.multiple_of((2 * i + 1 - core) * own, GROUP), own)].astype(BF)
-    k_copies = launch([to_expert(ksend, krecv, k_send.at[0], k_recv.at[0], 1)])
-    arrive(k_copies)
+    send(ksend, krecv, k_sems, 1)
+    k_moved = group(ksend, k_sems)
+    arrive(k_moved)
     for i in range(n // 2):
         red[i] = acc[pl.ds(pl.multiple_of((2 * i + core) * own, GROUP), own)] + krecv[i].astype(F32)
     for k in range(1, m):
         there = flip(mz, k, m)
         psend[k] = red[:, :, pl.ds(pl.multiple_of(there * cols, 128), cols)].astype(BF)
-    z_copies = launch(to_dp(lambda k: psend.at[k], lambda k: precv.at[k], z_send, z_recv))
+    to_dp(lambda k: psend.at[k], lambda k: precv.at[k], z_sems)
+    z_moved = group(psend.at[pl.ds(1, m - 1)], z_sems)
 
     def token_grads(b, carry):
         gt[b] = jnp.dot(gcf[b].T.astype(BF), allp[...], preferred_element_type=F32).astype(BF)
         return carry
 
     lax.fori_loop(0, imgs, token_grads, 0)
-    arrive(z_copies)
+    arrive(z_moved)
     total = red[:, :, my_cols]
     for k in range(1, m):
         total = total + precv[k].astype(F32)
     red[:, :, my_cols] = total
     for k in range(2, n, 2):
         xsend[k // 2] = red[flip(me, k, n) // 2, :, my_cols].astype(BF)
-    x_copies = launch([
-        to_expert(xsend.at[k // 2], xrecv.at[k // 2], x_send.at[k], x_recv.at[k], k) for k in range(2, n, 2)
-    ])
+    for k in range(2, n, 2):
+        send(xsend.at[k // 2], xrecv.at[k // 2], x_sems, k)
+    x_moved = group(xsend.at[pl.ds(1, n // 2 - 1)], x_sems)
     return_grads(1, (chunks - 1,))
-    for keep in keeps:
-        keep.wait()
+    for j in range(chunks):
+        every = all_grads(j, 2)
+        pltpu.make_async_copy(every, every, keep_sem.at[j]).wait()
     for j in range(chunks - 1):
-        grads_moved(j).wait_recv()
+        arrive(g_moved[j])
 
         def swap(c, carry):
             lanes = pl.ds(pl.multiple_of(c * LANES, LANES), LANES)
@@ -523,16 +563,14 @@
             return carry
 
         lax.fori_loop(0, width // LANES, swap, 0)
-    arrive(x_copies)
+    arrive(x_moved)
     owned = red[me // 2, :, my_cols]
     for k in range(2, n, 2):
         owned = owned + xrecv[k // 2].astype(F32)
     gp[...] = owned
-    for copy in sent:
-        copy.wait_send()
-    for j in range(chunks):
-        grads_moved(j).wait_send()
-    grads_moved(chunks - 1).wait_recv()
+    for moved in groups:
+        moved.wait_send()
+    arrive(g_moved[chunks - 1])
 
 
 def paired_exchange(n, m, tok, go, so, par):
@@ -575,12 +613,9 @@
             pltpu.VMEM((m, n // 2, own, cols), BF),
             pltpu.VMEM((n // 2, own, cols), BF),
             pltpu.VMEM((n // 2, own, cols), BF),
-            dma((4,)), dma((2, 2, own // GROUP)),
-            dma((n,)), dma((n,)), dma((n // 2, m)), dma((n // 2, m)),
-            dma((n // 2,)), dma((n // 2,)), dma((1,)), dma((1,)),
-            dma((2,)), dma((2,)), dma((2, 3)), dma((2, 3)), dma((2,)), dma((2,)),
-            dma((2,)), dma((2,)), dma((own // GROUP,)), dma((own // GROUP,)),
-            dma((m,)), dma((m,)), dma((n,)), dma((n,)),
+            pltpu.SemaphoreType.REGULAR, pltpu.SemaphoreType.REGULAR, dma((4,)), dma((own // GROUP,)),
+            dma((2,)), dma((n // 2, 2)), dma((2,)), dma((2,)), dma((2,)), dma((2,)), dma((2,)),
+            dma((2,)), dma((own // GROUP, 2)), dma((2,)), dma((2,)),
         ],
         compiler_params=pltpu.CompilerParams(
             collective_id=0, has_side_effects=True, vmem_limit_bytes=56 * 1000 * 1000
@@ -610,23 +645,30 @@
 
 def finish_kernel(done, last, gt, gp, slot_out, tok_out, par_out, turned, sem):
     own = done.shape[0]
-    copies = [
-        pltpu.make_async_copy(done, slot_out.at[pl.ds(0, own)], sem.at[0]),
-        pltpu.make_async_copy(gt, tok_out, sem.at[1]),
-        pltpu.make_async_copy(gp, par_out, sem.at[2]),
-    ]
-    for copy in copies:
-        copy.start()
     group, all_img, width = turned.shape
-
-    def swap(c, carry):
-        lanes = pl.ds(pl.multiple_of(c * LANES, LANES), LANES)
-        turned[:, :, lanes] = jnp.swapaxes(last[:, :, :, lanes].reshape(all_img, group, LANES), 0, 1)
-        return carry
-
-    lax.fori_loop(0, width // LANES, swap, 0)
-    copies.append(pltpu.make_async_copy(turned, slot_out.at[pl.ds(own, group)], sem.at[3]))
-    copies[3].start()
+    copies = []
+
+    def put(src, dst, at):
+        copies.append(pltpu.make_async_copy(src, dst, sem.at[at]))
+        copies[-1].start()
+
+    for g in range(own // group):
+        rows = pl.ds(g * group, group)
+        put(done.at[rows], slot_out.at[rows], 0)
+    for b in range(gt.shape[0]):
+        put(gt.at[b], tok_out.at[b], 1)
+    put(gp, par_out, 2)
+    tiles = width // LANES
+    for part in range(2):
+
+        def swap(c, carry):
+            lanes = pl.ds(pl.multiple_of((part * (tiles // 2) + c) * LANES, LANES), LANES)
+            turned[:, :, lanes] = jnp.swapaxes(last[:, :, :, lanes].reshape(all_img, group, LANES), 0, 1)
+            return carry
+
+        lax.fori_loop(0, tiles // 2, swap, 0)
+        lanes = pl.ds(part * (width // 2), width // 2)
+        put(turned.at[:, :, lanes], slot_out.at[pl.ds(own, group), :, lanes], 3)
     for copy in copies:
         copy.wait()
 

time: 133 us -> 131 us (0.985)
  Pallas kernels: 132 us -> 130 us
    pallas_call x1, Pallas kernels: 128 us -> 126 us  [paired_exchange(): pl.pallas_call(functools.partial(paired_kernel, n, m), out_shape=(pltpu.V...]
where the time goes in v2:
time: 131 us; the launch traced here: 130 us
  Pallas kernels  130 us (99%)
    pallas_call x1, Pallas kernels, paired_exchange(): pl.pallas_call(functools.partial(paired_kernel, n, m), out_shape=(pltpu.V...  126 us
    pallas_call x1, Pallas kernels, finish(): pl.pallas_call(finish_kernel, out_shape=(jax.ShapeDtypeStruct((own + GROU...  3.67 us

profile of v2, /device:TPU:0, one launch (start us, length us, event | category | flops | bytes accessed | tf_op | source)
XLA Modules:
  0.0 130.5 jit_solution(3558949763309323017)
XLA Ops:
  0.6 126.1 %shard_map.67 = (bf16[48,48,1024]{2,1,0:T(8,128)(2,1)S(1)}, bf16[8,6,16,1024]{3,2,1,0:T(8,128)(2,1)S(1)}, bf16[6,256,1024]{2,1,0:T(8,128)(2,1)S(1)}, f32[64,256]{1,0:T(8,128)S(1)}) custom-call(bf16[6,256,1024]{2,1,0:T(8,128)(2,1)} %bitcast.3, bf16[6,256,1024]{2,1,0:T(8,128)(2,1)} %bitcast.4, bf16[64,48,1024]{2,1,0:T(8,128)(2,1)} %so_hbm.1, ...), custom_call_target="tpu_custom_call" | custom-call | tf_op jit(solution)/shard_map/pallas_call | solution.py:581
  126.8 3.7 %shard_map.68 = (bf16[64,48,1024]{2,1,0:T(8,128)(2,1)}, bf16[6,256,1024]{2,1,0:T(8,128)(2,1)}, f32[64,256]{1,0:T(8,128)}) custom-call(bf16[48,48,1024]{2,1,0:T(8,128)(2,1)S(1)} %get-tuple-element.10.done, bf16[8,6,16,1024]{3,2,1,0:T(8,128)(2,1)S(1)} %get-tuple-element.11.last, bf16[6,256,1024]{2,1,0:T(8,128)(2,1)S(1)} %get-tuple-element.12.gt, ...), custom_call_target="tpu_custom_call" | custom-call | tf_op jit(solution)/shard_map/pallas_call | solution.py:678

commit v3 on v2

--- a/solution.py
+++ b/solution.py
@@ -236,7 +236,6 @@
     )(tok, go, so, par)
 
 
-NEAR = (1, 2, 3, 4, 5)
 AXES = ((2, (4, 5, 1)), (4, (2, 3, 1)))
 
 
@@ -250,8 +249,8 @@
     done, last, gt, gp,
     tok, go, mate, so, par, allp, stage, rows, gs, comb, gcf, low, low_send, gc_send, gc_recv,
     grec, acc, ksend, krecv, red, psend, precv, xsend, xrecv,
-    ready, corner, local_sem, keep_sem, p_sems, q_sems, f_sems, k_sems, o_sems, a_sems, w_sems,
-    c_sems, g_sems, z_sems, x_sems,
+    ready, corner, planes, local_sem, keep_sem, p_sems, r_sems, q_sems, f_sems, k_sems, o_sems, a_sems, w_sems,
+    c_sems, g_sems, z_sems, x_sems, y_sems,
 ):
     me = lax.axis_index("expert")
     mz = lax.axis_index("dp")
@@ -272,12 +271,13 @@
         start = p * 2 * quarter + side * quarter if which == 0 else side * 2 * quarter + p * quarter
         return pl.ds(pl.multiple_of(start, quarter), quarter)
 
-    loads = [
-        pltpu.make_async_copy(src, dst, local_sem.at[i])
-        for i, (src, dst) in enumerate([(par_hbm, par), (so_hbm, so), (tok_hbm, tok), (go_hbm, go)])
-    ]
-    for i in (0, 3, 1, 2):
-        loads[i].start()
+    def load(src, dst, at):
+        copy = pltpu.make_async_copy(src, dst, local_sem.at[at])
+        copy.start()
+        return copy
+
+    par_load = load(par_hbm, par, 0)
+    go_loads = [load(go_hbm.at[q * half], go.at[q * half], 1 + q) for q in range(2)]
 
     gate = n - 1
     barrier = pltpu.get_barrier_semaphore()
@@ -285,44 +285,52 @@
     def tell(sem, plane, index):
         pl.semaphore_signal(sem, inc=1, device_id=(plane, index), device_id_type=pl.DeviceIdType.MESH)
 
-    for k in NEAR:
-
-        @pl.when(flip(me, k, n) != gate)
-        def greet():
-            tell(barrier, mz, flip(me, k, n))
+    partner = flip(me, 1, n)
+    along_y = flip(me, 4, n) // 2 * 2 + 1
+    tell(barrier, mz, flip(me, 2, n) // 2 * 2)
+    tell(barrier, mz, jnp.where(along_y == gate, gate - 1, along_y))
+
+    @pl.when(partner != gate)
+    def greet():
+        tell(barrier, mz, partner)
+
+    @pl.when(me < gate - 1)
+    def meet():
+        pl.semaphore_wait(barrier, 3)
+
+    @pl.when(me == gate - 1)
+    def meet_all():
+        pl.semaphore_wait(barrier, 5)
 
     @pl.when(me != gate)
-    def meet():
-        pl.semaphore_wait(barrier, len(NEAR))
-
-    @pl.when(me == gate - 1)
-    def admit():
-        tell(ready, mz, gate)
+    def pass_on():
+        tell(ready, mz, partner)
 
     @pl.when(me == gate)
     def enter():
         pl.semaphore_wait(ready, 1)
 
-    tell(corner, mz, flip(me, 2, n))
-
-    def meet_corner():
+    def meet_side():
+        @pl.when(me < gate - 1)
+        def side():
+            pl.semaphore_wait(ready, 1)
+
+        tell(corner, mz, flip(me, 2, n))
+
+    def meet_planes():
         pl.semaphore_wait(corner, 1)
 
         @pl.when(me == gate)
-        def announce():
+        def spread():
             for k in range(1, m):
                 tell(barrier, flip(mz, k, m), gate)
-
-    def meet_planes():
-        @pl.when(me == gate)
-        def spread():
             pl.semaphore_wait(barrier, m - 1)
             for k in range(1, n):
-                tell(ready, mz, flip(me, k, n))
+                tell(planes, mz, flip(me, k, n))
 
         @pl.when(me != gate)
         def follow():
-            pl.semaphore_wait(ready, 1)
+            pl.semaphore_wait(planes, 1)
 
     def to_expert(src, dst, send, recv, k):
         return pltpu.make_async_remote_copy(
@@ -349,22 +357,38 @@
     def arrive(moved):
         moved.wait_recv()
 
-    loads[0].wait()
-    def send_params(peers):
-        for k in peers:
-            send(par.at[:, my_cols], allp.at[my_rows, my_cols], p_sems, k)
-
-    send_params((2, 4))
-    loads[3].wait()
-    for q in range(2):
-        send(go.at[pl.ds(q * half, half)], mate.at[q], o_sems, AXES[q][0])
+    def rows_of(mask, start, size):
+        return pl.ds(pl.multiple_of(flip(me, mask, n) * own + start, GROUP), size)
+
+    def send_params(q):
+        send(par.at[:, my_cols], allp.at[my_rows, my_cols], p_sems, 2 + 2 * q)
+
+    def send_first(q):
+        send(go.at[q * half], mate.at[q, 0], o_sems, 2 + 2 * q)
+
+    par_load.wait()
+    send_params(me % 2)
+    for copy in go_loads:
+        copy.wait()
+    send_first(me % 2)
+    meet_side()
+    send_params(1 - me % 2)
+    send_first(1 - me % 2)
+    rest = [pl.ds(q * half + 1, half - 1) for q in range(2)]
+    rest_loads = [load(go_hbm.at[part], go.at[part], 3 + q) for q, part in enumerate(rest)]
+    so_load = load(so_hbm, so, 5)
+    tok_load = load(tok_hbm, tok, 6)
+    allp[my_rows, my_cols] = par[:, my_cols]
+    arrive(group(allp.at[pl.ds(0, 2 * own), my_cols], p_sems))
+    for q in range(2):
+        block = allp.at[rows_of(4 - 2 * q, (1 - q) * (own // 2), own // 2), my_cols]
+        send(block, block, r_sems, AXES[q][0])
+        rest_loads[q].wait()
+        send(go.at[rest[q]], mate.at[q, pl.ds(1, half - 1)], o_sems, AXES[q][0])
+    r_moved = group(allp.at[pl.ds(0, own), my_cols], r_sems)
     o_moved = group(mate, o_sems)
-    meet_corner()
-    send_params((6,))
-    p_moved = group(allp.at[pl.ds(0, 3 * own), my_cols], p_sems)
-    allp[my_rows, my_cols] = par[:, my_cols]
-
-    loads[1].wait()
+
+    so_load.wait()
     out_r = lax.broadcasted_iota(jnp.int32, (imgs * GROUP, GROUP * all_img), 0)
     in_c = lax.broadcasted_iota(jnp.int32, (imgs * GROUP, GROUP * all_img), 1)
     base = in_c - (out_r % GROUP) * all_img - (out_r // GROUP) % half
@@ -393,17 +417,17 @@
     for q in range(2):
         relayout(q, me, rows.at[q, side_spot(q, me)])
 
-    arrive(p_moved)
+    arrive(r_moved)
     meet_planes()
     for i in range(n // 2):
-        block = allp.at[pl.ds(pl.multiple_of(flip(me, 2 * i, n) * own, GROUP), own), my_cols]
+        block = allp.at[rows_of(2 * i, 0, own), my_cols]
         to_dp(lambda k: block, lambda k: block, q_sems.at[i])
     q_moved = [group(precv.at[pl.ds(1, m - 1), 0], q_sems.at[i]) for i in range(n // 2)]
-    loads[2].wait()
+    tok_load.wait()
     for moved in q_moved:
         arrive(moved)
     for i in range(n // 2):
-        block = allp.at[pl.ds(pl.multiple_of(flip(me, 2 * i, n) * own, GROUP), own)]
+        block = allp.at[rows_of(2 * i, 0, own)]
         send(block, block, f_sems, 1)
     f_moved = group(allp.at[pl.ds(0, n // 2 * own)], f_sems)
     arrive(f_moved)
@@ -459,10 +483,10 @@
             return last.at[holder, images]
         return grec.at[holder, images, pl.ds(j * GROUP, GROUP)]
 
-    def return_grads(h, parts):
+    def return_grads(h, parts, steps=(0, 1, 2)):
         part = pl.ds(h * half, half)
         for j in parts:
-            for i in range(3):
+            for i in steps:
                 for q in range(2):
                     k = AXES[q][1][i]
                     holder = flip(me, AXES[q][0], n) if h else me
@@ -470,7 +494,7 @@
                         gs.at[q, side_spot(q, flip(me, k, n)), part, pl.ds(j * GROUP, GROUP)],
                         landing(holder, pl.ds(q * half, half), j), g_sems.at[j], k,
                     )
-            for q in range(2):
+            for q in range(2 if 2 in steps else 0):
                 holder = flip(me, AXES[q][0], n) if h else me
                 pltpu.make_async_copy(
                     gs.at[q, side_spot(q, me), part, pl.ds(j * GROUP, GROUP)],
@@ -491,7 +515,7 @@
             return carry
 
         lax.fori_loop(0, half, mate_slots, 0)
-    return_grads(1, range(chunks - 1))
+    return_grads(1, range(chunks - 2))
 
     for q in range(2):
 
@@ -544,16 +568,21 @@
     for k in range(1, m):
         total = total + precv[k].astype(F32)
     red[:, :, my_cols] = total
-    for k in range(2, n, 2):
-        xsend[k // 2] = red[flip(me, k, n) // 2, :, my_cols].astype(BF)
-    for k in range(2, n, 2):
-        send(xsend.at[k // 2], xrecv.at[k // 2], x_sems, k)
-    x_moved = group(xsend.at[pl.ds(1, n // 2 - 1)], x_sems)
-    return_grads(1, (chunks - 1,))
-    for j in range(chunks):
+
+    def share(mask, q):
+        return flip(me, mask, n) // 2, slice(q * (own // 2), (q + 1) * (own // 2)), my_cols
+
+    for q in range(2):
+        for i, mask in enumerate((AXES[q][0], 6)):
+            xsend[q, i] = red[share(mask, q)].astype(BF)
+        send(xsend.at[q, pl.ds(0, 2)], xrecv.at[q, pl.ds(0, 2)], x_sems, AXES[q][0])
+    x_moved = group(xsend.at[:, pl.ds(0, 2)], x_sems)
+    return_grads(1, (chunks - 2,))
+    return_grads(1, (chunks - 1,), (0,))
+
+    def settle_grads(j):
         every = all_grads(j, 2)
         pltpu.make_async_copy(every, every, keep_sem.at[j]).wait()
-    for j in range(chunks - 1):
         arrive(g_moved[j])
 
         def swap(c, carry):
@@ -563,11 +592,24 @@
             return carry
 
         lax.fori_loop(0, width // LANES, swap, 0)
+
+    for j in range(chunks - 3):
+        settle_grads(j)
     arrive(x_moved)
-    owned = red[me // 2, :, my_cols]
-    for k in range(2, n, 2):
-        owned = owned + xrecv[k // 2].astype(F32)
-    gp[...] = owned
+    for q in range(2):
+        for i, mask in enumerate((0, 4 - 2 * q)):
+            red[share(mask, q)] += xrecv[q, i].astype(F32)
+        xsend[q, 2] = red[share(4 - 2 * q, q)].astype(BF)
+        send(xsend.at[q, 2], xrecv.at[q, 2], y_sems, 4 - 2 * q)
+    y_moved = group(xsend.at[:, 2], y_sems)
+    return_grads(1, (chunks - 1,), (1, 2))
+    for j in range(chunks - 3, chunks - 1):
+        settle_grads(j)
+    arrive(y_moved)
+    for q in range(2):
+        gp[q * (own // 2) : (q + 1) * (own // 2)] = red[share(0, q)] + xrecv[q, 2].astype(F32)
+    every = all_grads(chunks - 1, 2)
+    pltpu.make_async_copy(every, every, keep_sem.at[chunks - 1]).wait()
     for moved in groups:
         moved.wait_send()
     arrive(g_moved[chunks - 1])
@@ -611,11 +653,11 @@
             pltpu.VMEM((n // 2, own, width), F32),
             pltpu.VMEM((m, n // 2, own, cols), BF),
             pltpu.VMEM((m, n // 2, own, cols), BF),
-            pltpu.VMEM((n // 2, own, cols), BF),
-            pltpu.VMEM((n // 2, own, cols), BF),
-            pltpu.SemaphoreType.REGULAR, pltpu.SemaphoreType.REGULAR, dma((4,)), dma((own // GROUP,)),
-            dma((2,)), dma((n // 2, 2)), dma((2,)), dma((2,)), dma((2,)), dma((2,)), dma((2,)),
-            dma((2,)), dma((own // GROUP, 2)), dma((2,)), dma((2,)),
+            pltpu.VMEM((2, 3, own // 2, cols), BF),
+            pltpu.VMEM((2, 3, own // 2, cols), BF),
+            pltpu.SemaphoreType.REGULAR, pltpu.SemaphoreType.REGULAR, pltpu.SemaphoreType.REGULAR,
+            dma((7,)), dma((own // GROUP,)), dma((2,)), dma((2,)), dma((n // 2, 2)), dma((2,)), dma((2,)), dma((2,)), dma((2,)), dma((2,)),
+            dma((2,)), dma((own // GROUP, 2)), dma((2,)), dma((2,)), dma((2,)),
         ],
         compiler_params=pltpu.CompilerParams(
             collective_id=0, has_side_effects=True, vmem_limit_bytes=56 * 1000 * 1000
@@ -692,7 +734,7 @@
 def per_device(n, m, tokens, grad_out, slot_out, slot_params):
     tok = jnp.transpose(tokens, (1, 0, 2))
     go = jnp.transpose(grad_out, (1, 0, 2))
-    if n == 8 and tok.shape[0] % 2 == 0:
+    if n == 8 and tok.shape[0] % 2 == 0 and tok.shape[0] > 2:
         grad_slot, grad_tok, grad_par = finish(*paired_exchange(n, m, tok, go, slot_out, slot_params))
     else:
         arrived, grad_tok, grad_par = exchange(n, m, tok, go, slot_out, slot_params)

time: 131 us -> 130 us (level)
  no operation moved by 1% of the time
where the time goes in v3:
time: 130 us
  Pallas kernels  130 us (100%)
    pallas_call x1, Pallas kernels, paired_exchange(): pl.pallas_call(functools.partial(paired_kernel, n, m), out_shape=(pltpu.V...  126 us
    pallas_call x1, Pallas kernels, finish(): pl.pallas_call(finish_kernel, out_shape=(jax.ShapeDtypeStruct((own + GROU...  3.67 us

profile of v3, /device:TPU:0, one launch (start us, length us, event | category | flops | bytes accessed | tf_op | source)
XLA Modules:
  0.0 130.3 jit_solution(2788002418399003067)
XLA Ops:
  0.6 126.0 %shard_map.67 = (bf16[48,48,1024]{2,1,0:T(8,128)(2,1)S(1)}, bf16[8,6,16,1024]{3,2,1,0:T(8,128)(2,1)S(1)}, bf16[6,256,1024]{2,1,0:T(8,128)(2,1)S(1)}, f32[64,256]{1,0:T(8,128)S(1)}) custom-call(bf16[6,256,1024]{2,1,0:T(8,128)(2,1)} %bitcast.3, bf16[6,256,1024]{2,1,0:T(8,128)(2,1)} %bitcast.4, bf16[64,48,1024]{2,1,0:T(8,128)(2,1)} %so_hbm.1, ...), custom_call_target="tpu_custom_call" | custom-call | tf_op jit(solution)/shard_map/pallas_call | solution.py:623
  126.6 3.7 %shard_map.68 = (bf16[64,48,1024]{2,1,0:T(8,128)(2,1)}, bf16[6,256,1024]{2,1,0:T(8,128)(2,1)}, f32[64,256]{1,0:T(8,128)}) custom-call(bf16[48,48,1024]{2,1,0:T(8,128)(2,1)S(1)} %get-tuple-element.10.done, bf16[8,6,16,1024]{3,2,1,0:T(8,128)(2,1)S(1)} %get-tuple-element.11.last, bf16[6,256,1024]{2,1,0:T(8,128)(2,1)S(1)} %get-tuple-element.12.gt, ...), custom_call_target="tpu_custom_call" | custom-call | tf_op jit(solution)/shard_map/pallas_call | solution.py:720

commit v4 on v3

--- a/solution.py
+++ b/solution.py
@@ -247,7 +247,7 @@
 def paired_kernel(
     n, m, tok_hbm, go_hbm, so_hbm, par_hbm,
     done, last, gt, gp,
-    tok, go, mate, so, par, allp, stage, rows, gs, comb, gcf, low, low_send, gc_send, gc_recv,
+    tok, go, mate, so, allp, stage, rows, gs, comb, gcf, low, low_send, gc_send, gc_recv,
     grec, acc, ksend, krecv, red, psend, precv, xsend, xrecv,
     ready, corner, planes, local_sem, keep_sem, p_sems, r_sems, q_sems, f_sems, k_sems, o_sems, a_sems, w_sems,
     c_sems, g_sems, z_sems, x_sems, y_sems,
@@ -256,7 +256,7 @@
     mz = lax.axis_index("dp")
     imgs = tok.shape[0]
     half = imgs // 2
-    own = par.shape[0]
+    own = par_hbm.shape[0]
     all_img = so.shape[1]
     slots, width = allp.shape
     patches = tok.shape[1]
@@ -276,8 +276,7 @@
         copy.start()
         return copy
 
-    par_load = load(par_hbm, par, 0)
-    go_loads = [load(go_hbm.at[q * half], go.at[q * half], 1 + q) for q in range(2)]
+    par_load = load(par_hbm.at[:, my_cols], allp.at[my_rows, my_cols], 0)
 
     gate = n - 1
     barrier = pltpu.get_barrier_semaphore()
@@ -360,31 +359,21 @@
     def rows_of(mask, start, size):
         return pl.ds(pl.multiple_of(flip(me, mask, n) * own + start, GROUP), size)
 
-    def send_params(q):
-        send(par.at[:, my_cols], allp.at[my_rows, my_cols], p_sems, 2 + 2 * q)
-
-    def send_first(q):
-        send(go.at[q * half], mate.at[q, 0], o_sems, 2 + 2 * q)
-
-    par_load.wait()
-    send_params(me % 2)
-    for copy in go_loads:
-        copy.wait()
-    send_first(me % 2)
+    def open_axis(q):
+        send(par_hbm.at[:, my_cols], allp.at[my_rows, my_cols], p_sems, 2 + 2 * q)
+        send(go_hbm.at[q * half], mate.at[q, 0], o_sems, 2 + 2 * q)
+
+    open_axis(me % 2)
     meet_side()
-    send_params(1 - me % 2)
-    send_first(1 - me % 2)
-    rest = [pl.ds(q * half + 1, half - 1) for q in range(2)]
-    rest_loads = [load(go_hbm.at[part], go.at[part], 3 + q) for q, part in enumerate(rest)]
-    so_load = load(so_hbm, so, 5)
-    tok_load = load(tok_hbm, tok, 6)
-    allp[my_rows, my_cols] = par[:, my_cols]
+    open_axis(1 - me % 2)
+    so_load = load(so_hbm, so, 1)
+    go_load = load(go_hbm, go, 2)
     arrive(group(allp.at[pl.ds(0, 2 * own), my_cols], p_sems))
     for q in range(2):
         block = allp.at[rows_of(4 - 2 * q, (1 - q) * (own // 2), own // 2), my_cols]
         send(block, block, r_sems, AXES[q][0])
-        rest_loads[q].wait()
-        send(go.at[rest[q]], mate.at[q, pl.ds(1, half - 1)], o_sems, AXES[q][0])
+        send(go_hbm.at[pl.ds(q * half + 1, half - 1)], mate.at[q, pl.ds(1, half - 1)], o_sems, AXES[q][0])
+    tok_load = load(tok_hbm, tok, 3)
     r_moved = group(allp.at[pl.ds(0, own), my_cols], r_sems)
     o_moved = group(mate, o_sems)
 
@@ -417,15 +406,16 @@
     for q in range(2):
         relayout(q, me, rows.at[q, side_spot(q, me)])
 
+    par_load.wait()
     arrive(r_moved)
     meet_planes()
     for i in range(n // 2):
         block = allp.at[rows_of(2 * i, 0, own), my_cols]
-        to_dp(lambda k: block, lambda k: block, q_sems.at[i])
-    q_moved = [group(precv.at[pl.ds(1, m - 1), 0], q_sems.at[i]) for i in range(n // 2)]
+        to_dp(lambda k: block, lambda k: block, q_sems)
+    q_moved = group(precv.at[pl.ds(1, m - 1)], q_sems)
+    go_load.wait()
     tok_load.wait()
-    for moved in q_moved:
-        arrive(moved)
+    arrive(q_moved)
     for i in range(n // 2):
         block = allp.at[rows_of(2 * i, 0, own)]
         send(block, block, f_sems, 1)
@@ -635,7 +625,6 @@
             pltpu.VMEM((imgs, patches, width), BF),
             pltpu.VMEM((2, half, patches, width), BF),
             pltpu.VMEM((own, all_img, width), BF),
-            pltpu.VMEM((own, width), BF),
             pltpu.VMEM((slots, width), BF),
             pltpu.VMEM((2, 3, imgs, own, width), BF),
             pltpu.VMEM((2, 4, imgs, own, width), BF),
@@ -656,7 +645,7 @@
             pltpu.VMEM((2, 3, own // 2, cols), BF),
             pltpu.VMEM((2, 3, own // 2, cols), BF),
             pltpu.SemaphoreType.REGULAR, pltpu.SemaphoreType.REGULAR, pltpu.SemaphoreType.REGULAR,
-            dma((7,)), dma((own // GROUP,)), dma((2,)), dma((2,)), dma((n // 2, 2)), dma((2,)), dma((2,)), dma((2,)), dma((2,)), dma((2,)),
+            dma((4,)), dma((own // GROUP,)), dma((2,)), dma((2,)), dma((2,)), dma((2,)), dma((2,)), dma((2,)), dma((2,)), dma((2,)),
             dma((2,)), dma((own // GROUP, 2)), dma((2,)), dma((2,)), dma((2,)),
         ],
         compiler_params=pltpu.CompilerParams(

time: 130 us -> 130 us (level)
  no operation moved by 1% of the time
where the time goes in v4:
time: 130 us
  Pallas kernels  129 us (99%)
    pallas_call x1, Pallas kernels, paired_exchange(): pl.pallas_call(functools.partial(paired_kernel, n, m), out_shape=(pltpu.V...  125 us
    pallas_call x1, Pallas kernels, finish(): pl.pallas_call(finish_kernel, out_shape=(jax.ShapeDtypeStruct((own + GROU...  3.67 us

profile of v4, /device:TPU:0, one launch (start us, length us, event | category | flops | bytes accessed | tf_op | source)
XLA Modules:
  0.0 129.6 jit_solution(927373202660378405)
XLA Ops:
  0.6 125.3 %shard_map.67 = (bf16[48,48,1024]{2,1,0:T(8,128)(2,1)S(1)}, bf16[8,6,16,1024]{3,2,1,0:T(8,128)(2,1)S(1)}, bf16[6,256,1024]{2,1,0:T(8,128)(2,1)S(1)}, f32[64,256]{1,0:T(8,128)S(1)}) custom-call(bf16[6,256,1024]{2,1,0:T(8,128)(2,1)} %bitcast.3, bf16[6,256,1024]{2,1,0:T(8,128)(2,1)} %bitcast.4, bf16[64,48,1024]{2,1,0:T(8,128)(2,1)} %so_hbm.1, ...), custom_call_target="tpu_custom_call" | custom-call | tf_op jit(solution)/shard_map/pallas_call | solution.py:613
  125.9 3.7 %shard_map.68 = (bf16[64,48,1024]{2,1,0:T(8,128)(2,1)}, bf16[6,256,1024]{2,1,0:T(8,128)(2,1)}, f32[64,256]{1,0:T(8,128)}) custom-call(bf16[48,48,1024]{2,1,0:T(8,128)(2,1)S(1)} %get-tuple-element.10.done, bf16[8,6,16,1024]{3,2,1,0:T(8,128)(2,1)S(1)} %get-tuple-element.11.last, bf16[6,256,1024]{2,1,0:T(8,128)(2,1)S(1)} %get-tuple-element.12.gt, ...), custom_call_target="tpu_custom_call" | custom-call | tf_op jit(solution)/shard_map/pallas_call | solution.py:709

commit v5 on v4

--- a/solution.py
+++ b/solution.py
@@ -285,9 +285,11 @@
         pl.semaphore_signal(sem, inc=1, device_id=(plane, index), device_id_type=pl.DeviceIdType.MESH)
 
     partner = flip(me, 1, n)
-    along_y = flip(me, 4, n) // 2 * 2 + 1
-    tell(barrier, mz, flip(me, 2, n) // 2 * 2)
-    tell(barrier, mz, jnp.where(along_y == gate, gate - 1, along_y))
+    high = me // 4
+    early = (me + high + 1) % 2
+    for mask in (2, 4):
+        host = flip(me, mask, n) // 2 * 2 + 1 - high
+        tell(barrier, mz, jnp.where(host == gate, gate - 1, host))
 
     @pl.when(partner != gate)
     def greet():
@@ -363,9 +365,9 @@
         send(par_hbm.at[:, my_cols], allp.at[my_rows, my_cols], p_sems, 2 + 2 * q)
         send(go_hbm.at[q * half], mate.at[q, 0], o_sems, 2 + 2 * q)
 
-    open_axis(me % 2)
+    open_axis(early)
     meet_side()
-    open_axis(1 - me % 2)
+    open_axis(1 - early)
     so_load = load(so_hbm, so, 1)
     go_load = load(go_hbm, go, 2)
     arrive(group(allp.at[pl.ds(0, 2 * own), my_cols], p_sems))

time: 130 us -> 129 us (level)
  no operation moved by 1% of the time
where the time goes in v5:
time: 129 us
  Pallas kernels  128 us (99%)
    pallas_call x1, Pallas kernels, paired_exchange(): pl.pallas_call(functools.partial(paired_kernel, n, m), out_shape=(pltpu.V...  125 us
    pallas_call x1, Pallas kernels, finish(): pl.pallas_call(finish_kernel, out_shape=(jax.ShapeDtypeStruct((own + GROU...  3.67 us

profile of v5, /device:TPU:0, one launch (start us, length us, event | category | flops | bytes accessed | tf_op | source)
XLA Modules:
  0.0 129.0 jit_solution(1856244794648940234)
XLA Ops:
  0.6 124.7 %shard_map.67 = (bf16[48,48,1024]{2,1,0:T(8,128)(2,1)S(1)}, bf16[8,6,16,1024]{3,2,1,0:T(8,128)(2,1)S(1)}, bf16[6,256,1024]{2,1,0:T(8,128)(2,1)S(1)}, f32[64,256]{1,0:T(8,128)S(1)}) custom-call(bf16[6,256,1024]{2,1,0:T(8,128)(2,1)} %bitcast.3, bf16[6,256,1024]{2,1,0:T(8,128)(2,1)} %bitcast.4, bf16[64,48,1024]{2,1,0:T(8,128)(2,1)} %so_hbm.1, ...), custom_call_target="tpu_custom_call" | custom-call | tf_op jit(solution)/shard_map/pallas_call | solution.py:615
  125.3 3.7 %shard_map.68 = (bf16[64,48,1024]{2,1,0:T(8,128)(2,1)}, bf16[6,256,1024]{2,1,0:T(8,128)(2,1)}, f32[64,256]{1,0:T(8,128)}) custom-call(bf16[48,48,1024]{2,1,0:T(8,128)(2,1)S(1)} %get-tuple-element.10.done, bf16[8,6,16,1024]{3,2,1,0:T(8,128)(2,1)S(1)} %get-tuple-element.11.last, bf16[6,256,1024]{2,1,0:T(8,128)(2,1)S(1)} %get-tuple-element.12.gt, ...), custom_call_target="tpu_custom_call" | custom-call | tf_op jit(solution)/shard_map/pallas_call | solution.py:711

commit v6 on v5

--- a/solution.py
+++ b/solution.py
@@ -249,8 +249,8 @@
     done, last, gt, gp,
     tok, go, mate, so, allp, stage, rows, gs, comb, gcf, low, low_send, gc_send, gc_recv,
     grec, acc, ksend, krecv, red, psend, precv, xsend, xrecv,
-    ready, corner, planes, local_sem, keep_sem, p_sems, r_sems, q_sems, f_sems, k_sems, o_sems, a_sems, w_sems,
-    c_sems, g_sems, z_sems, x_sems, y_sems,
+    ready, corner, planes, local_sem, keep_sem, p_sems, q_sems, f_sems, o_sems, a_sems, w_sems,
+    g_sems, z_sems, x_sems,
 ):
     me = lax.axis_index("expert")
     mz = lax.axis_index("dp")
@@ -346,8 +346,8 @@
                 device_id=(flip(mz, k, m), me), device_id_type=pl.DeviceIdType.MESH,
             ).start()
 
-    def send(src, dst, sems, k):
-        to_expert(src, dst, sems.at[0], sems.at[1], k).start()
+    def send(src, dst, sems, k, at=1):
+        to_expert(src, dst, sems.at[0], sems.at[at], k).start()
 
     groups = []
 
@@ -355,6 +355,9 @@
         groups.append(to_expert(every, every, sems.at[0], sems.at[1], 1))
         return groups[-1]
 
+    def landed(every, sems, at):
+        return to_expert(every, every, sems.at[0], sems.at[at], 1)
+
     def arrive(moved):
         moved.wait_recv()
 
@@ -363,20 +366,20 @@
 
     def open_axis(q):
         send(par_hbm.at[:, my_cols], allp.at[my_rows, my_cols], p_sems, 2 + 2 * q)
-        send(go_hbm.at[q * half], mate.at[q, 0], o_sems, 2 + 2 * q)
+        send(go_hbm.at[pl.ds(q * half, half)], mate.at[q], o_sems, 2 + 2 * q)
 
     open_axis(early)
     meet_side()
     open_axis(1 - early)
     so_load = load(so_hbm, so, 1)
     go_load = load(go_hbm, go, 2)
-    arrive(group(allp.at[pl.ds(0, 2 * own), my_cols], p_sems))
+    arrive(landed(allp.at[pl.ds(0, 2 * own), my_cols], p_sems, 1))
     for q in range(2):
         block = allp.at[rows_of(4 - 2 * q, (1 - q) * (own // 2), own // 2), my_cols]
-        send(block, block, r_sems, AXES[q][0])
-        send(go_hbm.at[pl.ds(q * half + 1, half - 1)], mate.at[q, pl.ds(1, half - 1)], o_sems, AXES[q][0])
+        send(block, block, p_sems, AXES[q][0], 2)
     tok_load = load(tok_hbm, tok, 3)
-    r_moved = group(allp.at[pl.ds(0, own), my_cols], r_sems)
+    r_moved = landed(allp.at[pl.ds(0, own), my_cols], p_sems, 2)
+    group(allp.at[pl.ds(0, 3 * own), my_cols], p_sems)
     o_moved = group(mate, o_sems)
 
     so_load.wait()
@@ -421,7 +424,7 @@
     for i in range(n // 2):
         block = allp.at[rows_of(2 * i, 0, own)]
         send(block, block, f_sems, 1)
-    f_moved = group(allp.at[pl.ds(0, n // 2 * own)], f_sems)
+    f_moved = landed(allp.at[pl.ds(0, n // 2 * own)], f_sems, 1)
     arrive(f_moved)
 
     for q in range(2):
@@ -439,7 +442,7 @@
 
         lax.fori_loop(0, half, forward, 0)
         send(low_send.at[q], low.at[q, pl.ds(half, half)], w_sems, AXES[q][0])
-    w_moved = group(low_send, w_sems)
+    w_moved = landed(low_send, w_sems, 1)
 
     def slot_grads(q, i, grads_in):
         out = jnp.dot(low[q, i], grads_in, preferred_element_type=F32).astype(BF)
@@ -465,8 +468,9 @@
             return carry
 
         lax.fori_loop(0, half, mate_comb, 0)
-        send(gc_send.at[q], gc_recv.at[q], c_sems, AXES[q][0])
-    c_moved = group(gc_send, c_sems)
+        send(gc_send.at[q], gc_recv.at[q], w_sems, AXES[q][0], 2)
+    c_moved = landed(gc_send, w_sems, 2)
+    group(low, w_sems)
 
     chunks = own // GROUP
 
@@ -484,19 +488,20 @@
                     holder = flip(me, AXES[q][0], n) if h else me
                     send(
                         gs.at[q, side_spot(q, flip(me, k, n)), part, pl.ds(j * GROUP, GROUP)],
-                        landing(holder, pl.ds(q * half, half), j), g_sems.at[j], k,
+                        landing(holder, pl.ds(q * half, half), j), g_sems, k, 1 + j,
                     )
             for q in range(2 if 2 in steps else 0):
                 holder = flip(me, AXES[q][0], n) if h else me
                 pltpu.make_async_copy(
                     gs.at[q, side_spot(q, me), part, pl.ds(j * GROUP, GROUP)],
-                    landing(holder, pl.ds(q * half, half), j), keep_sem.at[j],
+                    landing(holder, pl.ds(q * half, half), j), keep_sem.at[j // (chunks - 1)],
                 ).start()
 
     def all_grads(j, holders):
         return last.at[:holders] if j == chunks - 1 else grec.at[:holders, :, pl.ds(j * GROUP, GROUP)]
 
-    g_moved = [group(all_grads(j, n - 2), g_sems.at[j]) for j in range(chunks)]
+    g_moved = [landed(all_grads(j, n - 2), g_sems, 1 + j) for j in range(chunks)]
+    group(gs.at[:, pl.ds(0, 3)], g_sems)
 
     return_grads(0, range(chunks))
     arrive(w_moved)
@@ -539,8 +544,9 @@
     core = me % 2
     for i in range(n // 2):
         ksend[i] = acc[pl.ds(pl.multiple_of((2 * i + 1 - core) * own, GROUP), own)].astype(BF)
-    send(ksend, krecv, k_sems, 1)
-    k_moved = group(ksend, k_sems)
+    send(ksend, krecv, f_sems, 1, 2)
+    k_moved = landed(ksend, f_sems, 2)
+    group(allp, f_sems)
     arrive(k_moved)
     for i in range(n // 2):
         red[i] = acc[pl.ds(pl.multiple_of((2 * i + core) * own, GROUP), own)] + krecv[i].astype(F32)
@@ -568,13 +574,11 @@
         for i, mask in enumerate((AXES[q][0], 6)):
             xsend[q, i] = red[share(mask, q)].astype(BF)
         send(xsend.at[q, pl.ds(0, 2)], xrecv.at[q, pl.ds(0, 2)], x_sems, AXES[q][0])
-    x_moved = group(xsend.at[:, pl.ds(0, 2)], x_sems)
+    x_moved = landed(xsend.at[:, pl.ds(0, 2)], x_sems, 1)
     return_grads(1, (chunks - 2,))
     return_grads(1, (chunks - 1,), (0,))
 
     def settle_grads(j):
-        every = all_grads(j, 2)
-        pltpu.make_async_copy(every, every, keep_sem.at[j]).wait()
         arrive(g_moved[j])
 
         def swap(c, carry):
@@ -585,6 +589,7 @@
 
         lax.fori_loop(0, width // LANES, swap, 0)
 
+    pltpu.make_async_copy(grec.at[:2], grec.at[:2], keep_sem.at[0]).wait()
     for j in range(chunks - 3):
         settle_grads(j)
     arrive(x_moved)
@@ -592,8 +597,9 @@
         for i, mask in enumerate((0, 4 - 2 * q)):
             red[share(mask, q)] += xrecv[q, i].astype(F32)
         xsend[q, 2] = red[share(4 - 2 * q, q)].astype(BF)
-        send(xsend.at[q, 2], xrecv.at[q, 2], y_sems, 4 - 2 * q)
-    y_moved = group(xsend.at[:, 2], y_sems)
+        send(xsend.at[q, 2], xrecv.at[q, 2], x_sems, 4 - 2 * q, 2)
+    y_moved = landed(xsend.at[:, 2], x_sems, 2)
+    group(xsend, x_sems)
     return_grads(1, (chunks - 1,), (1, 2))
     for j in range(chunks - 3, chunks - 1):
         settle_grads(j)
@@ -601,7 +607,7 @@
     for q in range(2):
         gp[q * (own // 2) : (q + 1) * (own // 2)] = red[share(0, q)] + xrecv[q, 2].astype(F32)
     every = all_grads(chunks - 1, 2)
-    pltpu.make_async_copy(every, every, keep_sem.at[chunks - 1]).wait()
+    pltpu.make_async_copy(every, every, keep_sem.at[1]).wait()
     for moved in groups:
         moved.wait_send()
     arrive(g_moved[chunks - 1])
@@ -647,8 +653,8 @@
             pltpu.VMEM((2, 3, own // 2, cols), BF),
             pltpu.VMEM((2, 3, own // 2, cols), BF),
             pltpu.SemaphoreType.REGULAR, pltpu.SemaphoreType.REGULAR, pltpu.SemaphoreType.REGULAR,
-            dma((4,)), dma((own // GROUP,)), dma((2,)), dma((2,)), dma((2,)), dma((2,)), dma((2,)), dma((2,)), dma((2,)), dma((2,)),
-            dma((2,)), dma((own // GROUP, 2)), dma((2,)), dma((2,)), dma((2,)),
+            dma((4,)), dma((2,)), dma((3,)), dma((2,)), dma((3,)), dma((2,)), dma((2,)), dma((3,)),
+            dma((own // GROUP + 1,)), dma((2,)), dma((3,)),
         ],
         compiler_params=pltpu.CompilerParams(
             collective_id=0, has_side_effects=True, vmem_limit_bytes=56 * 1000 * 1000

time: 129 us -> 129 us (level)
  no operation moved by 1% of the time
where the time goes in v6:
time: 129 us
  Pallas kernels  128 us (99%)
    pallas_call x1, Pallas kernels, paired_exchange(): pl.pallas_call(functools.partial(paired_kernel, n, m), out_shape=(pltpu.V...  125 us
    pallas_call x1, Pallas kernels, finish(): pl.pallas_call(finish_kernel, out_shape=(jax.ShapeDtypeStruct((own + GROU...  3.67 us

profile of v6, /device:TPU:0, one launch (start us, length us, event | category | flops | bytes accessed | tf_op | source)
XLA Modules:
  0.0 128.9 jit_solution(719656946178301993)
XLA Ops:
  0.6 124.6 %shard_map.67 = (bf16[48,48,1024]{2,1,0:T(8,128)(2,1)S(1)}, bf16[8,6,16,1024]{3,2,1,0:T(8,128)(2,1)S(1)}, bf16[6,256,1024]{2,1,0:T(8,128)(2,1)S(1)}, f32[64,256]{1,0:T(8,128)S(1)}) custom-call(bf16[6,256,1024]{2,1,0:T(8,128)(2,1)} %bitcast.3, bf16[6,256,1024]{2,1,0:T(8,128)(2,1)} %bitcast.4, bf16[64,48,1024]{2,1,0:T(8,128)(2,1)} %so_hbm.1, ...), custom_call_target="tpu_custom_call" | custom-call | tf_op jit(solution)/shard_map/pallas_call | solution.py:621
  125.2 3.7 %shard_map.68 = (bf16[64,48,1024]{2,1,0:T(8,128)(2,1)}, bf16[6,256,1024]{2,1,0:T(8,128)(2,1)}, f32[64,256]{1,0:T(8,128)}) custom-call(bf16[48,48,1024]{2,1,0:T(8,128)(2,1)S(1)} %get-tuple-element.10.done, bf16[8,6,16,1024]{3,2,1,0:T(8,128)(2,1)S(1)} %get-tuple-element.11.last, bf16[6,256,1024]{2,1,0:T(8,128)(2,1)S(1)} %get-tuple-element.12.gt, ...), custom_call_target="tpu_custom_call" | custom-call | tf_op jit(solution)/shard_map/pallas_call | solution.py:717

commit v7 on v6

--- a/solution.py
+++ b/solution.py
@@ -276,8 +276,6 @@
         copy.start()
         return copy
 
-    par_load = load(par_hbm.at[:, my_cols], allp.at[my_rows, my_cols], 0)
-
     gate = n - 1
     barrier = pltpu.get_barrier_semaphore()
 
@@ -366,17 +364,19 @@
 
     def open_axis(q):
         send(par_hbm.at[:, my_cols], allp.at[my_rows, my_cols], p_sems, 2 + 2 * q)
-        send(go_hbm.at[pl.ds(q * half, half)], mate.at[q], o_sems, 2 + 2 * q)
+        send(go_hbm.at[q * half], mate.at[q, 0], o_sems, 2 + 2 * q)
 
     open_axis(early)
     meet_side()
     open_axis(1 - early)
+    par_load = load(par_hbm.at[:, my_cols], allp.at[my_rows, my_cols], 0)
     so_load = load(so_hbm, so, 1)
     go_load = load(go_hbm, go, 2)
     arrive(landed(allp.at[pl.ds(0, 2 * own), my_cols], p_sems, 1))
     for q in range(2):
         block = allp.at[rows_of(4 - 2 * q, (1 - q) * (own // 2), own // 2), my_cols]
         send(block, block, p_sems, AXES[q][0], 2)
+        send(go_hbm.at[pl.ds(q * half + 1, half - 1)], mate.at[q, pl.ds(1, half - 1)], o_sems, AXES[q][0])
     tok_load = load(tok_hbm, tok, 3)
     r_moved = landed(allp.at[pl.ds(0, own), my_cols], p_sems, 2)
     group(allp.at[pl.ds(0, 3 * own), my_cols], p_sems)

time: 129 us -> 129 us (level)
  no operation moved by 1% of the time
where the time goes in v7:
time: 129 us
  Pallas kernels  128 us (99%)
    pallas_call x1, Pallas kernels, paired_exchange(): pl.pallas_call(functools.partial(paired_kernel, n, m), out_shape=(pltpu.V...  125 us
    pallas_call x1, Pallas kernels, finish(): pl.pallas_call(finish_kernel, out_shape=(jax.ShapeDtypeStruct((own + GROU...  3.67 us

profile of v7, /device:TPU:0, one launch (start us, length us, event | category | flops | bytes accessed | tf_op | source)
XLA Modules:
  0.0 128.9 jit_solution(6728477294768283278)
XLA Ops:
  0.6 124.6 %shard_map.67 = (bf16[48,48,1024]{2,1,0:T(8,128)(2,1)S(1)}, bf16[8,6,16,1024]{3,2,1,0:T(8,128)(2,1)S(1)}, bf16[6,256,1024]{2,1,0:T(8,128)(2,1)S(1)}, f32[64,256]{1,0:T(8,128)S(1)}) custom-call(bf16[6,256,1024]{2,1,0:T(8,128)(2,1)} %bitcast.3, bf16[6,256,1024]{2,1,0:T(8,128)(2,1)} %bitcast.4, bf16[64,48,1024]{2,1,0:T(8,128)(2,1)} %so_hbm.1, ...), custom_call_target="tpu_custom_call" | custom-call | tf_op jit(solution)/shard_map/pallas_call | solution.py:621
  125.2 3.7 %shard_map.68 = (bf16[64,48,1024]{2,1,0:T(8,128)(2,1)}, bf16[6,256,1024]{2,1,0:T(8,128)(2,1)}, f32[64,256]{1,0:T(8,128)}) custom-call(bf16[48,48,1024]{2,1,0:T(8,128)(2,1)S(1)} %get-tuple-element.10.done, bf16[8,6,16,1024]{3,2,1,0:T(8,128)(2,1)S(1)} %get-tuple-element.11.last, bf16[6,256,1024]{2,1,0:T(8,128)(2,1)S(1)} %get-tuple-element.12.gt, ...), custom_call_target="tpu_custom_call" | custom-call | tf_op jit(solution)/shard_map/pallas_call | solution.py:717
